TPU v7x, 32 devices: a whole 2x2x4 slice. The times are simulated.
32 devices in a mesh: dp: 2 (over x), tp: 4 (over z), cp: 4 (over y, core).
Axes of the slice: x: 2, y: 2, z: 4, core: 2. Of those that a mesh axis runs over, the one named last changes fastest.
Arguments:
- hidden: bfloat16 [4096, 5120], P(('dp', 'cp', 'tp')), parts along dimension 0
- positions: int32 [4096], P(('dp', 'cp', 'tp')), parts along dimension 0
- doc_ids: int32 [4096], P(('dp', 'cp', 'tp')), parts along dimension 0
- attn_gain: bfloat16 [5120], replicated
- mlp_gain: bfloat16 [5120], replicated
- w_query: bfloat16 [5120, 5120], P(None, 'tp')
- w_key: bfloat16 [5120, 1024], P(None, 'tp')
- w_value: bfloat16 [5120, 1024], P(None, 'tp')
- w_out: bfloat16 [5120, 5120], P('tp')
- w_gate: bfloat16 [5120, 27648], P(None, 'tp')
- w_up: bfloat16 [5120, 27648], P(None, 'tp')
- w_down: bfloat16 [27648, 5120], P('tp')
Outputs:
- output: bfloat16 [4096, 5120], P(('dp', 'cp', 'tp')), parts along dimension 0
There are 2 independent parts. A program takes and returns all parts, laid end to end along the dimension named above; an argument that names none is the same for every part.
All inputs are finite; a program needn't handle non-finite values.
Results may differ from a plain program's by a relative error of at most 0.0125486.
Values are sent between devices in bfloat16 or wider.
A program may use at most 1 GiB of HBM per device.

v0:
```python
import jax
import jax.numpy as jnp
from jax import lax
from jax.sharding import PartitionSpec as P

HEAD_DIM = 128
ROPE_BASE = 500000.0
NORM_EPS = 1e-5
NEG_BIG = -1e30


def rms_norm(values, gain_vec):
    wide_vals = values.astype(jnp.float32)
    inv_rms = lax.rsqrt(jnp.mean(wide_vals * wide_vals, axis=-1, keepdims=True) + NORM_EPS)
    return (wide_vals * inv_rms * gain_vec.astype(jnp.float32)).astype(jnp.bfloat16)


def rotary(vectors, positions):
    half_dim = vectors.shape[-1] // 2
    inv_freq = ROPE_BASE ** (-jnp.arange(half_dim, dtype=jnp.float32) * (2.0 / vectors.shape[-1]))
    angles = positions.astype(jnp.float32)[:, None] * inv_freq[None, :]
    cos_ang = jnp.cos(angles)[:, None, :]
    sin_ang = jnp.sin(angles)[:, None, :]
    first_half = vectors[..., :half_dim]
    second_half = vectors[..., half_dim:]
    return jnp.concatenate([first_half * cos_ang - second_half * sin_ang, second_half * cos_ang + first_half * sin_ang], axis=-1)


def block_attend(queries, key_blk, val_blk, query_pos, query_doc, key_pos, key_doc, softmax_state):
    row_max, row_sum, accum = softmax_state
    scores = jnp.einsum('qhgd,khd->hgqk', queries, key_blk, preferred_element_type=jnp.float32) * (HEAD_DIM ** -0.5)
    visible = (query_doc[:, None] == key_doc[None, :]) & (key_pos[None, :] <= query_pos[:, None])
    scores = jnp.where(visible, scores, NEG_BIG)
    new_max = jnp.maximum(row_max, jnp.max(scores, axis=-1))
    weights = jnp.where(visible, jnp.exp(scores - new_max[..., None]), 0.0)
    factor = jnp.exp(row_max - new_max)
    row_sum = row_sum * factor + jnp.sum(weights, axis=-1)
    accum = accum * factor[..., None] + jnp.einsum('hgqk,khd->hgqd', weights.astype(jnp.bfloat16), val_blk, preferred_element_type=jnp.float32)
    return new_max, row_sum, accum


def solution(mesh):
    cp_size = mesh.shape['cp']
    ring_perm = [(idx, (idx + 1) % cp_size) for idx in range(cp_size)]
    row_mat = P(('dp', 'cp', 'tp'), None)
    row_vec = P(('dp', 'cp', 'tp'))
    col_split = P(None, 'tp')
    row_split = P('tp', None)

    def local_layer(hidden, positions, doc_ids, attn_gain, mlp_gain, w_query, w_key, w_value, w_out, w_gate, w_up, w_down):
        q_local = w_query.shape[1] // HEAD_DIM
        kv_local = w_key.shape[1] // HEAD_DIM
        group_size = q_local // kv_local
        normed = rms_norm(hidden, attn_gain)
        normed_all = lax.all_gather(normed, 'tp', axis=0, tiled=True)
        pos_all = lax.all_gather(positions, 'tp', axis=0, tiled=True)
        doc_all = lax.all_gather(doc_ids, 'tp', axis=0, tiled=True)
        row_count = normed_all.shape[0]
        queries = rotary(jnp.dot(normed_all, w_query, preferred_element_type=jnp.float32).reshape(row_count, q_local, HEAD_DIM), pos_all).astype(jnp.bfloat16).reshape(row_count, kv_local, group_size, HEAD_DIM)
        key_own = rotary(jnp.dot(normed_all, w_key, preferred_element_type=jnp.float32).reshape(row_count, kv_local, HEAD_DIM), pos_all).astype(jnp.bfloat16)
        value_own = jnp.dot(normed_all, w_value, preferred_element_type=jnp.float32).astype(jnp.bfloat16).reshape(row_count, kv_local, HEAD_DIM)
        start_state = (jnp.full((kv_local, group_size, row_count), NEG_BIG, jnp.float32), jnp.zeros((kv_local, group_size, row_count), jnp.float32), jnp.zeros((kv_local, group_size, row_count, HEAD_DIM), jnp.float32))
        first_state = block_attend(queries, key_own, value_own, pos_all, doc_all, pos_all, doc_all, start_state)

        def ring_step(step_idx, ring_state):
            key_blk, val_blk, kpos_blk, kdoc_blk, softmax_state = ring_state
            key_blk = lax.ppermute(key_blk, 'cp', ring_perm)
            val_blk = lax.ppermute(val_blk, 'cp', ring_perm)
            kpos_blk = lax.ppermute(kpos_blk, 'cp', ring_perm)
            kdoc_blk = lax.ppermute(kdoc_blk, 'cp', ring_perm)
            softmax_state = block_attend(queries, key_blk, val_blk, pos_all, doc_all, kpos_blk, kdoc_blk, softmax_state)
            return key_blk, val_blk, kpos_blk, kdoc_blk, softmax_state

        ring_out = lax.fori_loop(0, cp_size - 1, ring_step, (key_own, value_own, pos_all, doc_all, first_state))
        row_max, row_sum, accum = ring_out[4]
        attn_mix = (accum / row_sum[..., None]).astype(jnp.bfloat16)
        attn_part = jnp.einsum('hgqd,hgde->qe', attn_mix, w_out.reshape(kv_local, group_size, HEAD_DIM, w_out.shape[1]), preferred_element_type=jnp.float32).astype(jnp.bfloat16)
        attn_sum = lax.psum_scatter(attn_part, 'tp', scatter_dimension=0, tiled=True)
        residual = (hidden.astype(jnp.float32) + attn_sum.astype(jnp.float32)).astype(jnp.bfloat16)
        normed_mlp = rms_norm(residual, mlp_gain)
        mlp_in = lax.all_gather(normed_mlp, 'tp', axis=0, tiled=True)
        gate_val = jnp.dot(mlp_in, w_gate, preferred_element_type=jnp.float32)
        up_val = jnp.dot(mlp_in, w_up, preferred_element_type=jnp.float32)
        gated = (jax.nn.silu(gate_val) * up_val).astype(jnp.bfloat16)
        down_part = jnp.dot(gated, w_down, preferred_element_type=jnp.float32).astype(jnp.bfloat16)
        down_sum = lax.psum_scatter(down_part, 'tp', scatter_dimension=0, tiled=True)
        return (residual.astype(jnp.float32) + down_sum.astype(jnp.float32)).astype(jnp.bfloat16)

    in_specs = (row_mat, row_vec, row_vec, P(None), P(None), col_split, col_split, col_split, row_split, col_split, col_split, row_split)
    return jax.shard_map(local_layer, mesh=mesh, in_specs=in_specs, out_specs=row_mat, check_vma=False)
```

profile of v0, /device:TPU:0, one launch (start us, length us, event | category | flops | bytes accessed | tf_op | source)
XLA Modules:
  0.0 654.1 jit_solution(6675220952151786422)
XLA Ops:
  9.1 2.8 fusion.29
  11.9 12.7 %all-gather = s32[4,1,128]{2,1,0:T(1,128)S(1)} all-gather(s32[1,1,128]{2,1,0:T(1,128)S(1)} %bitcast.110), channel_id=1, replica_groups=mesh['dp'=2,'tp'=4,'cp'=4] {'tp'}, dimensions={0}, use_global_device_ids=true | all-gather | bytes 2560 | tf_op jit(solution)/shard_map/all_gather | solution.py:56
  24.6 7.7 %all-gather.1 = s32[4,1,128]{2,1,0:T(1,128)S(1)} all-gather(s32[1,1,128]{2,1,0:T(1,128)S(1)} %bitcast.111), channel_id=1, replica_groups=mesh['dp'=2,'tp'=4,'cp'=4] {'tp'}, dimensions={0}, use_global_device_ids=true | all-gather | bytes 2560 | tf_op jit(solution)/shard_map/all_gather | solution.py:57
  34.8 77.5 %all-gather.5.cloned.1.call-done = bf16[512,5120]{1,0:T(8,128)(2,1)} async-done(((bf16[128,5120]{1,0:T(8,128)(2,1)}), bf16[512,5120]{1,0:T(8,128)(2,1)}) %all-gather.5.cloned.1.call-update) | async-done | bytes 5242896 | tf_op jit(solution)/shard_map/all_gather | solution.py:55
  112.4 4.0 convolution_convert_fusion
  117.3 13.9 %fusion.48 = f32[512,1280]{0,1:T(8,128)S(1)} fusion(bf16[512,5120]{1,0:T(8,128)(2,1)} %all-gather.5.cloned.1.call-done, bf16[5120,1280]{1,0:T(8,128)(2,1)} %param.19), kind=kOutput, calls=%fused_computation.72 | convolution fusion | flops 6710886400 | bytes 20971520 | tf_op jit(solution)/shard_map/dot_general | solution.py:59
  132.5 3.4 fusion.47
  142.8 2.1 fusion.17
  145.0 2.5 fusion.22
  147.6 5.1 fusion.35
  152.6 49.7 %while.22 = (s32[]{:T(128)}, bf16[512,2,128]{2,0,1:T(8,128)(2,1)S(1)}, bf16[512,2,128]{2,0,1:T(8,128)(2,1)S(1)}, s32[512]{0:T(512)S(1)}, s32[512]{0:T(512)S(1)},...) while((s32[]{:T(128)}, ...), condition=%wide.region_6.7_spmd, body=%wide.region_3.6_spmd.sunk | while | flops 1378363392 | bytes 64061772 | solution.py:74
  154.9 3.6 collective-permute-done.3
  158.8 2.1 fusion.80
  160.9 2.5 fusion.81
  163.6 4.1 multiply_add_fusion.5
  171.5 3.6 collective-permute-done.3
  175.3 2.1 fusion.80
  177.5 2.5 fusion.81
  180.1 4.1 multiply_add_fusion.5
  188.0 3.6 collective-permute-done.3
  191.9 2.1 fusion.80
  194.1 2.5 fusion.81
  196.7 4.1 multiply_add_fusion.5
  202.3 12.4 %bitcast_convert_fusion = bf16[512,5120]{1,0:T(8,128)(2,1)} fusion(bf16[2,5,128,5120]{3,2,1,0:T(8,128)(2,1)} %bitcast.112, f32[2,5,512,128]{3,2,1,0:T(8,128)} %get-tuple-element.63, f32[2,5,512]{2,1,0:T(8,128)S(1)} %get-tuple-element.64), kind=kOutput, calls=%fused_computation.21 | convolution fusion | flops 6714818560 | bytes 20992000 | tf_op jit(solution)/shard_map/hgqd,hgde->qe/dot_general | solution.py:77
  215.4 91.7 %reduce-scatter.3.cloned.1.call-done = bf16[128,5120]{1,0:T(8,128)(2,1)} async-done(((bf16[512,5120]{1,0:T(8,128)(2,1)}), bf16[128,5120]{1,0:T(8,128)(2,1)}) %reduce-scatter.3.cloned.1.call-update) | async-done | bytes 1310736 | tf_op jit(solution)/shard_map/reduce_scatter | solution.py:78
  308.9 2.9 fusion.33
  311.8 98.3 %all-gather.7.cloned.1.call-done = bf16[512,5120]{1,0:T(8,128)(2,1)} async-done(((bf16[128,5120]{1,0:T(8,128)(2,1)}), bf16[512,5120]{1,0:T(8,128)(2,1)}) %all-gather.7.cloned.1.call-update) | async-done | bytes 5242896 | tf_op jit(solution)/shard_map/all_gather | solution.py:81
  410.1 46.0 %fusion.49 = f32[512,6912]{1,0:T(8,128)} fusion(bf16[512,5120]{1,0:T(8,128)(2,1)} %all-gather.7.cloned.1.call-done, bf16[5120,6912]{1,0:T(8,128)(2,1)} %param.23), kind=kOutput, calls=%fused_computation.73 | convolution fusion | flops 36238786560 | bytes 90177536 | tf_op jit(solution)/shard_map/dot_general | solution.py:82
  456.2 49.0 %multiply_convert_fusion.clone.6 = bf16[512,6912]{1,0:T(8,128)(2,1)} fusion(f32[512,6912]{1,0:T(8,128)} %fusion.49, bf16[512,5120]{1,0:T(8,128)(2,1)} %all-gather.7.cloned.1.call-done, bf16[5120,6912]{1,0:T(8,128)(2,1)} %param.24), kind=kOutput, calls=%fused_computation.17.clone.clone.clone.clone.clone.1 | convolution fusion | flops 36260020224 | bytes 97255424 | tf_op jit(solution)/shard_map/dot_general | solution.py:83
  505.2 46.0 %fusion.20 = bf16[512,5120]{1,0:T(8,128)(2,1)} fusion(bf16[6912,5120]{1,0:T(8,128)(2,1)} %param.25, bf16[512,6912]{1,0:T(8,128)(2,1)} %multiply_convert_fusion.clone.6), kind=kOutput, calls=%fused_computation.25 | convolution fusion | flops 36241408000 | bytes 83099648 | tf_op jit(solution)/shard_map/dot_general | solution.py:85
  551.2 92.3 %reduce-scatter.5.cloned.1.call-done = bf16[128,5120]{1,0:T(8,128)(2,1)} async-done(((bf16[512,5120]{1,0:T(8,128)(2,1)}), bf16[128,5120]{1,0:T(8,128)(2,1)}) %reduce-scatter.5.cloned.1.call-update) | async-done | bytes 1310736 | tf_op jit(solution)/shard_map/reduce_scatter | solution.py:86
  643.6 3.8 fusion.34
  (113 shorter events, 29.1 us)
Async XLA Ops:
  6.5 105.8 %copy-start = (bf16[5120,256]{1,0:T(8,128)(2,1)S(1)}, bf16[5120,256]{1,0:T(8,128)(2,1)}, u32[]{:S(2)}) copy-start(bf16[5120,256]{1,0:T(8,128)(2,1)} %param.21) | copy-start | bytes 7864324
  6.5 5.4 copy-start.8
  6.5 18.1 %copy-start.9 = (s32[128]{0:T(128)S(1)}, s32[128]{0:T(128)}, u32[]{:S(2)}) copy-start(s32[128]{0:T(128)} %param.16) | copy-start | bytes 1540
  6.5 105.8 %all-gather.5.cloned.1.call-start = ((), (), s32[]{:S(2)}) async-start(), calls=%async_computation.2 | async-start | bytes 6553600 | tf_op jit(solution)/shard_map/all_gather | solution.py:55
  11.9 295.2 %reduce-scatter.3.cloned.1.call-start = ((), (), s32[]{:S(2)}) async-start(), calls=%async_computation.3 | async-start | bytes 6553600 | tf_op jit(solution)/shard_map/reduce_scatter | solution.py:78
  116.4 14.8 %copy-start.5 = (bf16[512,256]{0,1:T(8,128)(2,1)}, bf16[512,256]{0,1:T(8,128)(2,1)S(1)}, u32[]{:S(2)}) copy-start(bf16[512,256]{0,1:T(8,128)(2,1)S(1)} %convolution_convert_fusion) | copy-start | bytes 786436
  117.3 15.2 %copy-start.10 = (bf16[512,5120]{1,0:T(8,128)(2,1)S(1)}, bf16[512,5120]{1,0:T(8,128)(2,1)}, u32[]{:S(2)}) copy-start(bf16[512,5120]{1,0:T(8,128)(2,1)} %all-gather.5.cloned.1.call-done) | copy-start | bytes 15728644
  132.5 4.7 copy-start.3
  145.0 2.6 copy-start.6
  147.6 5.1 copy-start.4
  152.6 6.1 collective-permute-start
  152.6 5.8 collective-permute-start.3
  154.2 4.2 collective-permute-start.2
  154.2 9.3 %collective-permute-start.1 = (bf16[512,2,128]{2,0,1:T(8,128)(2,1)S(1)}, bf16[512,2,128]{2,0,1:T(8,128)(2,1)S(1)}, u32[]{:S(2)}, u32[]{:S(2)}) collective-permute-start(bf16[512,2,128]{2,0,1:T(8,128)(2,1)S(1)} %get-tuple-element.236), channel_id=1, source_target_pairs={{0,1},{1,2},{2,3},{3,0},{4,5},{5,6},{6,7},{7,4},{8,9},{9,10},{10,1... | collective-permute-start | bytes 786440 | tf_op jit(solution)/shard_map/while/body/eval_jaxpr/ppermute | solution.py:68
  160.9 2.6 copy-start.11
  167.7 1.5 copy-start.12
  169.2 6.1 collective-permute-start
  169.2 5.8 collective-permute-start.3
  170.8 4.2 collective-permute-start.2
  170.8 9.3 %collective-permute-start.1 = (bf16[512,2,128]{2,0,1:T(8,128)(2,1)S(1)}, bf16[512,2,128]{2,0,1:T(8,128)(2,1)S(1)}, u32[]{:S(2)}, u32[]{:S(2)}) collective-permute-start(bf16[512,2,128]{2,0,1:T(8,128)(2,1)S(1)} %get-tuple-element.236), channel_id=1, source_target_pairs={{0,1},{1,2},{2,3},{3,0},{4,5},{5,6},{6,7},{7,4},{8,9},{9,10},{10,1... | collective-permute-start | bytes 786440 | tf_op jit(solution)/shard_map/while/body/eval_jaxpr/ppermute | solution.py:68
  177.5 2.6 copy-start.11
  184.3 1.5 copy-start.12
  185.8 6.1 collective-permute-start
  185.8 5.8 collective-permute-start.3
  187.3 4.2 collective-permute-start.2
  187.4 9.3 %collective-permute-start.1 = (bf16[512,2,128]{2,0,1:T(8,128)(2,1)S(1)}, bf16[512,2,128]{2,0,1:T(8,128)(2,1)S(1)}, u32[]{:S(2)}, u32[]{:S(2)}) collective-permute-start(bf16[512,2,128]{2,0,1:T(8,128)(2,1)S(1)} %get-tuple-element.236), channel_id=1, source_target_pairs={{0,1},{1,2},{2,3},{3,0},{4,5},{5,6},{6,7},{7,4},{8,9},{9,10},{10,1... | collective-permute-start | bytes 786440 | tf_op jit(solution)/shard_map/while/body/eval_jaxpr/ppermute | solution.py:68
  194.0 2.6 copy-start.11
  200.8 1.5 copy-start.12
  214.7 92.4 %copy-start.2 = (bf16[128,5120]{1,0:T(8,128)(2,1)S(1)}, bf16[128,5120]{1,0:T(8,128)(2,1)}, u32[]{:S(2)}) copy-start(bf16[128,5120]{1,0:T(8,128)(2,1)} %param.14) | copy-start | bytes 3932164
  214.7 195.4 %all-gather.7.cloned.1.call-start = ((), (), s32[]{:S(2)}) async-start(), calls=%async_computation.4 | async-start | bytes 6553600 | tf_op jit(solution)/shard_map/all_gather | solution.py:81
  311.8 331.8 %reduce-scatter.5.cloned.1.call-start = ((), (), s32[]{:S(2)}) async-start(), calls=%async_computation.5 | async-start | bytes 6553600 | tf_op jit(solution)/shard_map/reduce_scatter | solution.py:86
  551.2 96.1 %copy-start.1 = (bf16[5120,256]{1,0:T(8,128)(2,1)S(1)}, bf16[5120,256]{1,0:T(8,128)(2,1)}, u32[]{:S(2)}) copy-start(bf16[5120,256]{1,0:T(8,128)(2,1)} %param.21) | copy-start | bytes 7864324
  (1 other events, 0.7 us)
Sparse Core Ops, SparseCore 0:
  12.0 100.3 all-gather.4
  214.8 92.1 reduce-scatter.2
  311.9 98.1 all-gather.6
  551.4 92.1 reduce-scatter.4
where the time goes:
time: 658 us; the launch traced here: 654 us
  waiting for transfers between devices  371 us (56%)
  matrix products  201 us (31%)
  other arithmetic  30.4 us (5%)
  blocking collectives  20.4 us (3%)
  between operations  13.6 us (2%)
  local copies, waits for them, and re-layouts  11.1 us (2%)
  starting transfers between devices  6.9 us (1%)
    all_gather x1, waiting for transfers between devices, local_layer(): mlp_in = lax.all_gather(normed_mlp, 'tp', axis=0, tiled=True)  98.3 us
    reduce_scatter x1, waiting for transfers between devices, local_layer(): lax.psum_scatter(down_part, 'tp', scatter_dimension=0, tiled=True)  92.3 us
    reduce_scatter x1, waiting for transfers between devices, local_layer(): lax.psum_scatter(attn_part, 'tp', scatter_dimension=0, tiled=True)  91.7 us
    all_gather x1, waiting for transfers between devices, local_layer(): normed_all = lax.all_gather(normed, 'tp', axis=0, tiled=True)  77.5 us
    dot_general x1, matrix products, local_layer(): up_val = jnp.dot(mlp_in, w_up, preferred_element_type=jnp.float32)  49 us
    dot_general x1, matrix products, local_layer(): gate_val = jnp.dot(mlp_in, w_gate, preferred_element_type=jnp.float32)  46 us
    dot_general x1, matrix products, local_layer(): jnp.dot(gated, w_down, preferred_element_type=jnp.float32)  46 us
    dot_general x4, matrix products, block_attend(): jnp.einsum('hgqk,khd->hgqd', weights.astype(jnp.bfloat16), val_blk, prefe...  17.5 us
  transfers between devices with their start and end apart: 16, of which 7 were waited for; matrix products, arithmetic and copies ran while one was open for 3% of the time, Pallas kernels for 0%

commit v1 on v0

v1 whole, which is shorter than its diff:
```python
import functools

import jax
import jax.numpy as jnp
from jax import lax
from jax.experimental import pallas as pl
from jax.experimental.pallas import tpu as pltpu
from jax.sharding import PartitionSpec as P

HEAD_DIM = 128
ROPE_BASE = 500000.0
NORM_EPS = 1e-5
NEG_BIG = -1e30
MESH = pl.DeviceIdType.MESH
BF16 = jnp.bfloat16
F32 = jnp.float32
VMEM_LIMIT = 67043328

TP = 4
ROWS = 128
DIM = 5120
KC = 512
NK = DIM // KC
CC = 256
NCC = DIM // CC
PER = KC // CC
FILL = 4


def tp_barrier(z):
    barrier = pltpu.get_barrier_semaphore()
    for peer in range(TP):
        @pl.when(z != peer)
        def _():
            pl.semaphore_signal(barrier, inc=1, device_id={"tp": peer}, device_id_type=MESH)
    pl.semaphore_wait(barrier, TP - 1)


def gather_tools(z, bg, r_right, r_left, s_right, s_left):
    def blk(origin, chunk):
        lane = pl.multiple_of((chunk % PER) * CC, CC)
        return bg.at[chunk // PER, pl.ds(pl.multiple_of(origin * ROWS, ROWS), ROWS), pl.ds(lane, CC)]

    def right(dist, chunk):
        ref = blk(z - dist, chunk)
        return pltpu.make_async_remote_copy(ref, ref, s_right.at[dist, chunk], r_right.at[dist, chunk],
                                            device_id={"tp": jnp.minimum(z + 1, TP - 1)}, device_id_type=MESH)

    def left(dist, chunk):
        ref = blk(z + dist, chunk)
        return pltpu.make_async_remote_copy(ref, ref, s_left.at[dist, chunk], r_left.at[dist, chunk],
                                            device_id={"tp": jnp.maximum(z - 1, 0)}, device_id_type=MESH)

    def got_right(dist, chunk):
        ref = blk(z - 1 - dist, chunk)
        return pltpu.make_async_remote_copy(ref, ref, s_right.at[dist, chunk], r_right.at[dist, chunk],
                                            device_id={"tp": jnp.maximum(z - 1, 0)}, device_id_type=MESH)

    def got_left(dist, chunk):
        ref = blk(z + 1 + dist, chunk)
        return pltpu.make_async_remote_copy(ref, ref, s_left.at[dist, chunk], r_left.at[dist, chunk],
                                            device_id={"tp": jnp.minimum(z + 1, TP - 1)}, device_id_type=MESH)

    def tick(t):
        @pl.when((z < TP - 1) & (t < NCC))
        def _():
            right(0, t).start()

        @pl.when((z > 0) & (t < NCC))
        def _():
            left(0, t).start()

        for d in (1, 2):
            c = t - d
            ok = (c >= 0) & (c < NCC)

            @pl.when(ok & (z < TP - 1) & (z >= d))
            def _():
                got_right(d - 1, c).wait_recv()
                right(d, c).start()

            @pl.when(ok & (z > 0) & (z + d <= TP - 1))
            def _():
                got_left(d - 1, c).wait_recv()
                left(d, c).start()

    def arrived(g):
        @pl.when(z == TP - 1)
        def _():
            for d in range(TP - 1):
                for k in range(PER):
                    got_right(d, g * PER + k).wait_recv()

        @pl.when(z == 0)
        def _():
            for d in range(TP - 1):
                for k in range(PER):
                    got_left(d, g * PER + k).wait_recv()

    def drain():
        def body(c, _):
            for d in range(TP - 1):
                @pl.when((z < TP - 1) & (z >= d))
                def _():
                    right(d, c).wait_send()

                @pl.when((z > 0) & (z + d <= TP - 1))
                def _():
                    left(d, c).wait_send()
            return 0
        lax.fori_loop(0, NCC, body, 0)

    return tick, arrived, drain


def norm_into(z, x_ref, gain_ref, bg):
    def body(i, _):
        r0 = pl.multiple_of(i * 16, 16)
        wide = x_ref[pl.ds(r0, 16), :].astype(F32)
        inv = lax.rsqrt(jnp.mean(wide * wide, axis=-1, keepdims=True) + NORM_EPS)
        out = (wide * inv * gain_ref[...].astype(F32)).astype(BF16)
        row = pl.multiple_of(z * ROWS + r0, 16)
        for g in range(NK):
            bg[g, pl.ds(row, 16), :] = out[:, g * KC:(g + 1) * KC]
        return 0
    lax.fori_loop(0, ROWS // 16, body, 0)


GATHER_SEMS = [pltpu.SemaphoreType.DMA((TP - 1, NCC))] * 4

QT = 2304
SLOTS = 4


def gate_up_kernel(n_tiles, x_ref, gain_ref, wg, wu, out_ref, bg, acc, wbuf, wsem, r_right, r_left, s_right, s_left):
    z = lax.axis_index("tp")
    total = NK * 2 * n_tiles

    def fetch(i, start):
        q = i % (2 * n_tiles)
        k0 = pl.multiple_of((i // (2 * n_tiles)) * KC, KC)
        n0 = pl.multiple_of((q % n_tiles) * QT, QT)
        slot = i % SLOTS

        @pl.when(q < n_tiles)
        def _():
            c = pltpu.make_async_copy(wg.at[pl.ds(k0, KC), pl.ds(n0, QT)], wbuf.at[slot], wsem.at[slot])
            c.start() if start else c.wait()

        @pl.when(q >= n_tiles)
        def _():
            c = pltpu.make_async_copy(wu.at[pl.ds(k0, KC), pl.ds(n0, QT)], wbuf.at[slot], wsem.at[slot])
            c.start() if start else c.wait()

    for i in range(SLOTS - 1):
        fetch(i, True)
    norm_into(z, x_ref, gain_ref, bg)
    tp_barrier(z)
    tick, arrived, drain = gather_tools(z, bg, r_right, r_left, s_right, s_left)
    tick(0)

    def zero(i, _):
        q = i // 16
        r0 = pl.multiple_of((i % 16) * 32, 32)
        acc[q, pl.ds(r0, 32), :] = jnp.zeros((32, QT), F32)
        return 0
    lax.fori_loop(0, 2 * n_tiles * 16, zero, 0)
    for t in range(1, FILL):
        tick(t)

    def step(u, _):
        tick(u + FILL)
        g = u // 2

        @pl.when(u % 2 == 0)
        def _():
            arrived(g)

        def tile(j, _):
            i = u * n_tiles + j
            fetch(i, False)

            @pl.when(i + SLOTS - 1 < total)
            def _():
                fetch(i + SLOTS - 1, True)
            q = i % (2 * n_tiles)
            acc[q] += jnp.dot(bg[g], wbuf[i % SLOTS], preferred_element_type=F32)
            return 0
        lax.fori_loop(0, n_tiles, tile, 0)
        return 0
    lax.fori_loop(0, 2 * NK, step, 0)

    def finish(i, _):
        r0 = pl.multiple_of(i * 16, 16)
        for j in range(n_tiles):
            gate = acc[j, pl.ds(r0, 16), :]
            up = acc[n_tiles + j, pl.ds(r0, 16), :]
            out_ref[pl.ds(r0, 16), j * QT:(j + 1) * QT] = (jax.nn.silu(gate) * up).astype(BF16)
        return 0
    lax.fori_loop(0, TP * ROWS // 16, finish, 0)
    drain()


def gate_up(x, gain, wg, wu):
    ffn = wg.shape[1]
    n_tiles = ffn // QT
    vm = pl.BlockSpec(memory_space=pltpu.VMEM)
    hbm = pl.BlockSpec(memory_space=pl.ANY)
    return pl.pallas_call(
        functools.partial(gate_up_kernel, n_tiles),
        out_shape=jax.ShapeDtypeStruct((TP * ROWS, ffn), BF16),
        in_specs=[vm, vm, hbm, hbm],
        out_specs=vm,
        scratch_shapes=[
            pltpu.VMEM((NK, TP * ROWS, KC), BF16),
            pltpu.VMEM((2 * n_tiles, TP * ROWS, QT), F32),
            pltpu.VMEM((SLOTS, KC, QT), BF16),
            pltpu.SemaphoreType.DMA((SLOTS,)),
        ] + GATHER_SEMS,
        compiler_params=pltpu.CompilerParams(collective_id=2, has_side_effects=True, vmem_limit_bytes=VMEM_LIMIT),
        name="gate_up",
    )(x, gain.reshape(1, -1), wg, wu)


def qkv_kernel(x_ref, gain_ref, pos_ref, wq, wk, wv, out_ref, pos_out, bg, wbuf, wsem, psend, precv, r_right, r_left, s_right, s_left):
    z = lax.axis_index("tp")
    nq, nkv = wq.shape[1], wk.shape[1]

    def fetch(g, start):
        k0 = pl.multiple_of(g * KC, KC)
        slot = g % 2
        for idx, (w, off, width) in enumerate(((wq, 0, nq), (wk, nq, nkv), (wv, nq + nkv, nkv))):
            c = pltpu.make_async_copy(w.at[pl.ds(k0, KC), :], wbuf.at[slot, :, pl.ds(off, width)], wsem.at[slot, idx])
            c.start() if start else c.wait()

    fetch(0, True)
    fetch(1, True)
    pos_out[z] = pos_ref[...]
    norm_into(z, x_ref, gain_ref, bg)
    tp_barrier(z)
    tick, arrived, drain = gather_tools(z, bg, r_right, r_left, s_right, s_left)

    def pos_copy(peer, origin):
        return pltpu.make_async_remote_copy(pos_ref, pos_out.at[origin], psend.at[peer], precv.at[origin],
                                            device_id={"tp": peer}, device_id_type=MESH)
    tick(0)
    for peer in range(TP):
        @pl.when(z != peer)
        def _():
            pos_copy(peer, z).start()
    out_ref[...] = jnp.zeros(out_ref.shape, F32)
    for t in range(1, FILL):
        tick(t)

    def step(g, _):
        for h in range(2):
            tick(g * 2 + h + FILL)
        arrived(g)
        fetch(g, False)
        out_ref[...] += jnp.dot(bg[g], wbuf[g % 2], preferred_element_type=F32)

        @pl.when(g + 2 < NK)
        def _():
            fetch(g + 2, True)
        return 0
    lax.fori_loop(0, NK, step, 0)
    for peer in range(TP):
        @pl.when(z != peer)
        def _():
            pos_copy(peer, z).wait_send()
            pos_copy(peer, peer).wait_recv()
    drain()


def qkv_proj(x, gain, pos, wq, wk, wv):
    width = wq.shape[1] + wk.shape[1] + wv.shape[1]
    vm = pl.BlockSpec(memory_space=pltpu.VMEM)
    hbm = pl.BlockSpec(memory_space=pl.ANY)
    return pl.pallas_call(
        qkv_kernel,
        out_shape=(jax.ShapeDtypeStruct((TP * ROWS, width), F32), jax.ShapeDtypeStruct((TP, 8, ROWS), jnp.int32)),
        in_specs=[vm, vm, vm, hbm, hbm, hbm],
        out_specs=(vm, vm),
        scratch_shapes=[
            pltpu.VMEM((NK, TP * ROWS, KC), BF16),
            pltpu.VMEM((2, KC, width), BF16),
            pltpu.SemaphoreType.DMA((2, 3)),
            pltpu.SemaphoreType.DMA((TP,)),
            pltpu.SemaphoreType.DMA((TP,)),
        ] + GATHER_SEMS,
        compiler_params=pltpu.CompilerParams(collective_id=1, has_side_effects=True, vmem_limit_bytes=VMEM_LIMIT),
        name="qkv_proj",
    )(x, gain.reshape(1, -1), jnp.broadcast_to(pos[None, :], (8, ROWS)), wq, wk, wv)


NC = 512
NN = DIM // NC


def scatter_kernel(lhs, w, res_ref, out_ref, part, from_left, from_right, wbuf, wsem, r_right, r_left, ssem):
    z = lax.axis_index("tp")

    def fetch(c):
        return pltpu.make_async_copy(w.at[:, pl.ds(pl.multiple_of(c * NC, NC), NC)], wbuf.at[c % 2], wsem.at[c % 2])

    fetch(0).start()
    fetch(1).start()
    tp_barrier(z)

    def send_right(c, dest):
        return pltpu.make_async_remote_copy(part.at[c, dest], from_left.at[c, dest - 1], ssem.at[c, dest], r_right.at[c, dest - 1],
                                            device_id={"tp": jnp.minimum(z + 1, TP - 1)}, device_id_type=MESH)

    def send_left(c, dest):
        return pltpu.make_async_remote_copy(part.at[c, dest], from_right.at[c, dest], ssem.at[c, dest], r_left.at[c, dest],
                                            device_id={"tp": jnp.maximum(z - 1, 0)}, device_id_type=MESH)

    def got_left(c, dest):
        return pltpu.make_async_remote_copy(part.at[c, dest], from_left.at[c, dest - 1], ssem.at[c, dest], r_right.at[c, dest - 1],
                                            device_id={"tp": jnp.maximum(z - 1, 0)}, device_id_type=MESH)

    def got_right(c, dest):
        return pltpu.make_async_remote_copy(part.at[c, dest], from_right.at[c, dest], ssem.at[c, dest], r_left.at[c, dest],
                                            device_id={"tp": jnp.minimum(z + 1, TP - 1)}, device_id_type=MESH)

    def step(t, _):
        @pl.when(t < NN)
        def _():
            fetch(t).wait()
            for half in range(2):
                cols = slice(half * NC // 2, (half + 1) * NC // 2)
                prod = jnp.dot(lhs[...], wbuf[t % 2, :, cols], preferred_element_type=F32).astype(BF16)
                for dest in range(TP):
                    part[t, dest, :, cols] = prod[dest * ROWS:(dest + 1) * ROWS]

            @pl.when(t + 2 < NN)
            def _():
                fetch(t + 2).start()

        cr = t - z
        ok_r = (cr >= 0) & (cr < NN)
        cl = t - (TP - 1 - z)
        ok_l = (cl >= 0) & (cl < NN)
        for k in range(TP - 1):
            dest = TP - 1 - k

            @pl.when(ok_r & (dest > z))
            def _():
                @pl.when(z > 0)
                def _():
                    got_left(cr, dest).wait_recv()
                    part[cr, dest] = (part[cr, dest].astype(F32) + from_left[cr, dest - 1].astype(F32)).astype(BF16)
                send_right(cr, dest).start()

            dst = k

            @pl.when(ok_l & (dst < z))
            def _():
                @pl.when(z < TP - 1)
                def _():
                    got_right(cl, dst).wait_recv()
                    part[cl, dst] = (part[cl, dst].astype(F32) + from_right[cl, dst].astype(F32)).astype(BF16)
                send_left(cl, dst).start()

        cf = t - (TP - 1)

        @pl.when(cf >= 0)
        def _():
            cols = pl.ds(pl.multiple_of(jnp.maximum(cf, 0) * NC, NC), NC)

            @pl.when(z > 0)
            def _():
                got_left(cf, z).wait_recv()
                part[cf, z] = (part[cf, z].astype(F32) + from_left[cf, z - 1].astype(F32)).astype(BF16)

            @pl.when(z < TP - 1)
            def _():
                got_right(cf, z).wait_recv()
                part[cf, z] = (part[cf, z].astype(F32) + from_right[cf, z].astype(F32)).astype(BF16)
            out_ref[:, cols] = (res_ref[:, cols].astype(F32) + part[cf, z].astype(F32)).astype(BF16)
        return 0
    lax.fori_loop(0, NN + TP - 1, step, 0)

    def drain(c, _):
        for dest in range(TP):
            @pl.when(dest > z)
            def _():
                send_right(c, max(dest, 1)).wait_send()

            @pl.when(dest < z)
            def _():
                send_left(c, min(dest, TP - 2)).wait_send()
        return 0
    lax.fori_loop(0, NN, drain, 0)


def scatter_proj(lhs, w, res, cid, name):
    depth = w.shape[0]
    vm = pl.BlockSpec(memory_space=pltpu.VMEM)
    hbm = pl.BlockSpec(memory_space=pl.ANY)
    return pl.pallas_call(
        scatter_kernel,
        out_shape=jax.ShapeDtypeStruct((ROWS, DIM), BF16),
        in_specs=[vm, hbm, vm],
        out_specs=vm,
        scratch_shapes=[
            pltpu.VMEM((NN, TP, ROWS, NC), BF16),
            pltpu.VMEM((NN, TP - 1, ROWS, NC), BF16),
            pltpu.VMEM((NN, TP - 1, ROWS, NC), BF16),
            pltpu.VMEM((2, depth, NC), BF16),
            pltpu.SemaphoreType.DMA((2,)),
            pltpu.SemaphoreType.DMA((NN, TP - 1)),
            pltpu.SemaphoreType.DMA((NN, TP - 1)),
            pltpu.SemaphoreType.DMA((NN, TP)),
        ],
        compiler_params=pltpu.CompilerParams(collective_id=cid, has_side_effects=True, vmem_limit_bytes=VMEM_LIMIT),
        name=name,
    )(lhs, w, res)


def rotary(vectors, positions):
    half_dim = vectors.shape[-1] // 2
    inv_freq = ROPE_BASE ** (-jnp.arange(half_dim, dtype=jnp.float32) * (2.0 / vectors.shape[-1]))
    angles = positions.astype(jnp.float32)[:, None] * inv_freq[None, :]
    cos_ang = jnp.cos(angles)[:, None, :]
    sin_ang = jnp.sin(angles)[:, None, :]
    first_half = vectors[..., :half_dim]
    second_half = vectors[..., half_dim:]
    return jnp.concatenate([first_half * cos_ang - second_half * sin_ang, second_half * cos_ang + first_half * sin_ang], axis=-1)


def block_attend(queries, key_blk, val_blk, query_pos, query_doc, key_pos, key_doc, softmax_state):
    row_max, row_sum, accum = softmax_state
    scores = jnp.einsum('qhgd,khd->hgqk', queries, key_blk, preferred_element_type=jnp.float32) * (HEAD_DIM ** -0.5)
    visible = (query_doc[:, None] <= key_doc[None, :]) & (key_doc[None, :] <= query_pos[:, None])
    scores = jnp.where(visible, scores, NEG_BIG)
    new_max = jnp.maximum(row_max, jnp.max(scores, axis=-1))
    weights = jnp.where(visible, jnp.exp(scores - new_max[..., None]), 0.0)
    factor = jnp.exp(row_max - new_max)
    row_sum = row_sum * factor + jnp.sum(weights, axis=-1)
    accum = accum * factor[..., None] + jnp.einsum('hgqk,khd->hgqd', weights.astype(jnp.bfloat16), val_blk, preferred_element_type=jnp.float32)
    return new_max, row_sum, accum


def solution(mesh):
    cp_size = mesh.shape['cp']
    ring_perm = [(idx, (idx + 1) % cp_size) for idx in range(cp_size)]
    row_mat = P(('dp', 'cp', 'tp'), None)
    row_vec = P(('dp', 'cp', 'tp'))
    col_split = P(None, 'tp')
    row_split = P('tp', None)
    pieces = 2 * cp_size * TP
    piece_rows = ROWS // 2

    def logical_rows(cp_idx):
        row = jnp.arange(TP * ROWS, dtype=jnp.int32)
        t, r = row // ROWS, row % ROWS
        k = cp_idx * TP + t
        piece = jnp.where(r < piece_rows, k, pieces - 1 - k)
        return piece * piece_rows + r % piece_rows

    def local_layer(hidden, positions, doc_ids, attn_gain, mlp_gain, w_query, w_key, w_value, w_out, w_gate, w_up, w_down):
        q_local = w_query.shape[1] // HEAD_DIM
        kv_local = w_key.shape[1] // HEAD_DIM
        group_size = q_local // kv_local
        qkv, pos_blk = qkv_proj(hidden, attn_gain, positions, w_query, w_key, w_value)
        pos_all = pos_blk[:, 0, :].reshape(-1)
        row_count = TP * ROWS
        nq, nkv = w_query.shape[1], w_key.shape[1]
        queries = rotary(qkv[:, :nq].reshape(row_count, q_local, HEAD_DIM), pos_all).astype(BF16).reshape(row_count, kv_local, group_size, HEAD_DIM)
        key_own = rotary(qkv[:, nq:nq + nkv].reshape(row_count, kv_local, HEAD_DIM), pos_all).astype(BF16)
        value_own = qkv[:, nq + nkv:].astype(BF16).reshape(row_count, kv_local, HEAD_DIM)
        cp_idx = lax.axis_index('cp')
        q_log = logical_rows(cp_idx)
        q_first = q_log - pos_all
        state = (jnp.full((kv_local, group_size, row_count), NEG_BIG, F32), jnp.zeros((kv_local, group_size, row_count), F32), jnp.zeros((kv_local, group_size, row_count, HEAD_DIM), F32))
        key_blk, val_blk = key_own, value_own
        for s in range(cp_size):
            src = lax.rem(cp_idx - s + cp_size, cp_size)
            state = block_attend(queries, key_blk, val_blk, q_log, q_first, None, logical_rows(src), state)
            if s + 1 < cp_size:
                key_blk = lax.ppermute(key_blk, 'cp', ring_perm)
                val_blk = lax.ppermute(val_blk, 'cp', ring_perm)
        row_max, row_sum, accum = state
        attn_mix = (accum / row_sum[..., None]).astype(BF16)
        attn_mix = attn_mix.transpose(2, 0, 1, 3).reshape(row_count, nq)
        residual = scatter_proj(attn_mix, w_out, hidden, 3, "out_proj")
        gated = gate_up(residual, mlp_gain, w_gate, w_up)
        return scatter_proj(gated, w_down, residual, 4, "down_proj")

    in_specs = (row_mat, row_vec, row_vec, P(None), P(None), col_split, col_split, col_split, row_split, col_split, col_split, row_split)
    return jax.shard_map(local_layer, mesh=mesh, in_specs=in_specs, out_specs=row_mat, check_vma=False)
```

time: 658 us -> 515 us (0.78)
  Pallas kernels: 0 us -> 410 us
  waiting for transfers between devices: 371 us -> 1.2 us
  matrix products: 201 us -> 43.6 us
  blocking collectives: 20.4 us -> 0 us
  between operations: 13.6 us -> 0.71 us
  other arithmetic: 30.4 us -> 23.5 us
    pallas_call x0 -> x4, Pallas kernels: none -> 410 us  [the longest x2 194 us: scatter_proj(): pl.pallas_call(scatter_kernel, out_shape=jax.ShapeDtypeStruct((ROWS, DIM)...]
    reduce_scatter x2 -> x0, waiting for transfers between devices: 184 us -> none  [the longest x1 92.3 us: local_layer(): lax.psum_scatter(down_part, 'tp', scatter_dimension=0, tiled=True)]
    all_gather x2 -> x0, waiting for transfers between devices: 176 us -> none  [the longest x1 98.3 us: local_layer(): mlp_in = lax.all_gather(normed_mlp, 'tp', axis=0, tiled=True)]
    dot_general x7 -> x0, matrix products: 175 us -> none  [the longest x1 49 us: local_layer(): up_val = jnp.dot(mlp_in, w_up, preferred_element_type=jnp.float32)]
    all_gather x2 -> x0, blocking collectives: 20.4 us -> none  [the longest x1 12.7 us: local_layer(): pos_all = lax.all_gather(positions, 'tp', axis=0, tiled=True)]
    convert_element_type x5 -> x0, other arithmetic: 10.1 us -> none  [the longest x2 5.64 us: rms_norm(): (wide_vals * inv_rms * gain_vec.astype(jnp.float32)).astype(jnp.bfloat16)]
    ppermute x12 -> x6, waiting for transfers between devices: 10.8 us -> 1.2 us  [the longest x3 1.2 us: local_layer(): key_blk = lax.ppermute(key_blk, 'cp', ring_perm)]
    dot_general x4, matrix products: 17.5 us -> 26.3 us  [block_attend(): jnp.einsum('hgqk,khd->hgqd', weights.astype(jnp.bfloat16), val_blk, prefe...]
  transfers between devices with their start and end apart: 16 -> 6, of which waited for: 7 -> 1; matrix products, arithmetic and copies ran while one was open for 3% -> 14% of each run, Pallas kernels for 0% -> 0%
where the time goes in v1:
time: 515 us; the launch traced here: 510 us
  Pallas kernels  410 us (80%)
  matrix products  43.6 us (8%)
  other arithmetic  23.5 us (5%)
  local copies, waits for them, and re-layouts  17.5 us (3%)
  starting transfers between devices  12.9 us (3%)
    pallas_call x2, Pallas kernels, scatter_proj(): pl.pallas_call(scatter_kernel, out_shape=jax.ShapeDtypeStruct((ROWS, DIM)...  194 us
    pallas_call x1, Pallas kernels, gate_up(): pl.pallas_call(functools.partial(gate_up_kernel, n_tiles), out_shape=jax....  117 us
    pallas_call x1, Pallas kernels, qkv_proj(): pl.pallas_call(qkv_kernel, out_shape=(jax.ShapeDtypeStruct((TP * ROWS, wi...  99.1 us
    dot_general x4, matrix products, block_attend(): jnp.einsum('hgqk,khd->hgqd', weights.astype(jnp.bfloat16), val_blk, prefe...  26.3 us
    reduce_sum x4, other arithmetic, block_attend(): row_sum = row_sum * factor + jnp.sum(weights, axis=-1)  18 us
    dot_general x4, matrix products, block_attend(): jnp.einsum('qhgd,khd->hgqk', queries, key_blk, preferred_element_type=jnp...  17.3 us
    ppermute x3, starting transfers between devices, local_layer(): key_blk = lax.ppermute(key_blk, 'cp', ring_perm)  12.9 us
  transfers between devices with their start and end apart: 6, of which 1 were waited for; matrix products, arithmetic and copies ran while one was open for 14% of the time, Pallas kernels for 0%

profile of v1, /device:TPU:0, one launch (start us, length us, event | category | flops | bytes accessed | tf_op | source)
XLA Modules:
  0.0 509.9 jit_solution(13603226878937091121)
XLA Ops:
  0.0 1.3 reshape.260.gain_ref
  1.3 1.2 broadcast_in_dim.39.pos_ref
  2.6 99.1 %qkv_proj.1 = (f32[512,1792]{1,0:T(8,128)}, s32[4,8,128]{2,1,0:T(8,128)}) custom-call(bf16[128,5120]{1,0:T(8,128)(2,1)} %res_ref.1, bf16[1,5120]{1,0:T(2,128)(2,1)} %reshape.260.gain_ref, s32[8,128]{1,0:T(8,128)} %broadcast_in_dim.39.pos_ref, bf16[5120,1280]{1,0:T(8,128)(2,1)} %wq.1, bf16[5120,256]{1,0:T(8,128)(2,1)} %wk.1, bf16[5120,256]{1,0:T(8,128)(2,1)} %wv.1), custom_call_target="tpu_custom_call" | custom-call | tf_op jit(solution)/shard_map/qkv_proj/pallas_call | solution.py:279
  101.7 1.1 slice.43
  102.9 0.9 copy.46
  103.7 1.1 slice.26
  107.4 0.9 pad_maximum_fusion.1
  108.2 1.6 collective-permute-start
  109.9 1.9 slice.29
  111.8 2.1 copy.41
  113.9 2.1 subtract_convert_fusion
  116.8 0.7 copy.43
  118.4 1.0 compare_and_fusion.3
  119.4 2.8 fusion
  123.4 6.7 %fusion.1 = (f32[2,5,512]{2,1,0:T(8,128)S(1)}, f32[2,512,512,5]{2,1,3,0:T(8,128)}) fusion(pred[512,512]{0,1:T(8,128)(4,1)S(1)} %get-tuple-element.27, bf16[512,2,5,128]{3,0,2,1:T(8,128)(2,1)S(1)} %pad_maximum_fusion, bf16[512,2,128]{2,0,1:T(8,128)(2,1)} %collective-permute-done), kind=kOutput, calls=%fused_computation.9 | convolution fusion | flops 678947840 | bytes 12341248 | tf_op jit(solution)/shard_map/qhgd,khd->hgqk/dot_general | solution.py:434
  130.2 1.2 collective-permute-done.2
  131.4 10.6 %collective-permute-start.4 = (bf16[512,2,128]{2,0,1:T(8,128)(2,1)S(1)}, bf16[512,2,128]{2,0,1:T(8,128)(2,1)S(1)}, u32[]{:S(2)}, u32[]{:S(2)}) collective-permute-start(bf16[512,2,128]{2,0,1:T(8,128)(2,1)S(1)} %collective-permute-done.2), channel_id=1, source_target_pairs={{0,1},{1,2},{2,3},{3,0},{4,5},{5,6},{6,7},{7,4},{8,9},{9,10},{10,1... | collective-permute-start | bytes 786440 | tf_op jit(solution)/shard_map/ppermute | solution.py:482
  142.0 5.6 %fusion.2 = (f32[2,5,512]{2,1,0:T(8,128)S(1)}, f32[2,512,512,5]{2,1,3,0:T(8,128)}) fusion(pred[512,512]{0,1:T(8,128)(4,1)S(1)} %get-tuple-element.25, bf16[512,2,5,128]{3,0,2,1:T(8,128)(2,1)S(1)} %pad_maximum_fusion, bf16[512,2,128]{2,0,1:T(8,128)(2,1)S(1)} %collective-permute-done.2), kind=kOutput, calls=%fused_computation.10 | convolution fusion | flops 678947840 | bytes 12341248 | tf_op jit(solution)/shard_map/qhgd,khd->hgqk/dot_general | solution.py:434
  147.7 2.1 fusion.3
  149.8 2.5 fusion.10
  152.3 6.5 %fusion.8 = f32[2,5,512]{2,1,0:T(8,128)S(1)} fusion(f32[2,512,512,5]{2,1,3,0:T(8,128)} %get-tuple-element.33, f32[2,5,512]{2,1,0:T(8,128)S(1)} %get-tuple-element.13, pred[512,512]{0,1:T(8,128)(4,1)S(1)} %get-tuple-element.25), kind=kLoop, calls=%fused_computation.16 | loop fusion | flops 13102080 | bytes 10788864 | tf_op jit(solution)/shard_map/reduce_sum | solution.py:440
  158.8 6.5 %fusion.6 = f32[2,5,512]{2,1,0:T(8,128)S(1)} fusion(f32[2,512,512,5]{2,1,3,0:T(8,128)} %get-tuple-element.35, f32[2,5,512]{2,1,0:T(8,128)S(1)} %get-tuple-element.14, pred[512,512]{0,1:T(8,128)(4,1)S(1)} %get-tuple-element.27), kind=kLoop, calls=%fused_computation.14 | loop fusion | flops 13102080 | bytes 10788864 | tf_op jit(solution)/shard_map/reduce_sum | solution.py:440
  165.3 2.5 fusion.4
  167.9 8.8 %fusion.14 = f32[2,5,512,128]{2,3,1,0:T(8,128)} fusion(f32[2,512,512,5]{2,1,3,0:T(8,128)} %get-tuple-element.33, f32[2,5,512]{2,1,0:T(8,128)S(1)} %get-tuple-element.13, pred[512,512]{0,1:T(8,128)(4,1)S(1)} %get-tuple-element.25, bf16[512,2,128]{0,2,1:T(8,128)(2,1)} %collective-permute-done.3), kind=kOutput, calls=%fused_computation.21 | convolution fusion | flops 684195840 | bytes 13651968 | tf_op jit(solution)/shard_map/hgqk,khd->hgqd/dot_general | solution.py:441
  176.7 8.7 %fusion.16 = f32[2,5,512,128]{2,3,1,0:T(8,128)} fusion(f32[2,512,512,5]{2,1,3,0:T(8,128)} %get-tuple-element.35, f32[2,5,512]{2,1,0:T(8,128)S(1)} %get-tuple-element.14, pred[512,512]{0,1:T(8,128)(4,1)S(1)} %get-tuple-element.27, bf16[512,2,128]{0,2,1:T(8,128)(2,1)} %collective-permute-done.1), kind=kOutput, calls=%fused_computation.22 | convolution fusion | flops 684195840 | bytes 13651968 | tf_op jit(solution)/shard_map/hgqk,khd->hgqd/dot_general | solution.py:441
  185.4 3.2 fusion.18
  188.7 5.5 %fusion.25 = bf16[512,2,5,128]{0,3,2,1:T(8,128)(2,1)S(1)} fusion(f32[2,5,512,128]{2,3,1,0:T(8,128)} %fusion.14, f32[2,5,512,128]{2,3,1,0:T(8,128)} %fusion.16, f32[2,5,512,128]{2,3,1,0:T(8,128)S(1)} %fusion.18, f32[2,512,512,5]{2,1,3,0:T(8,128)S(1)} %get-tuple-element.31, f32[2,5,512]{2,1,0:T(8,128)S(1)} %get-tuple-element.12, ...), kind=kOutput, calls=%fused_computation.30 | convolution fusion | flops 690094080 | bytes 20307968 | tf_op jit(solution)/shard_map/hgqk,khd->hgqd/dot_general | solution.py:441
  194.2 1.4 copy.50.lhs
  195.7 96.4 %out_proj.1.x_ref.res_ref = bf16[128,5120]{1,0:T(8,128)(2,1)} custom-call(bf16[512,1280]{1,0:T(8,128)(2,1)} %copy.50.lhs, bf16[1280,5120]{1,0:T(8,128)(2,1)} %w.2, bf16[128,5120]{1,0:T(8,128)(2,1)} %res_ref.1), custom_call_target="tpu_custom_call" | custom-call | tf_op jit(solution)/shard_map/out_proj/pallas_call | solution.py:401
  292.0 116.8 %gate_up.1.lhs = bf16[512,6912]{1,0:T(8,128)(2,1)} custom-call(bf16[128,5120]{1,0:T(8,128)(2,1)} %out_proj.1.x_ref.res_ref, bf16[1,5120]{1,0:T(2,128)(2,1)} %reshape.265.gain_ref, bf16[5120,6912]{1,0:T(8,128)(2,1)} %wg.1, bf16[5120,6912]{1,0:T(8,128)(2,1)} %wu.1), custom_call_target="tpu_custom_call" | custom-call | tf_op jit(solution)/shard_map/gate_up/pallas_call | solution.py:209
  408.8 98.1 %down_proj.1 = bf16[128,5120]{1,0:T(8,128)(2,1)} custom-call(bf16[512,6912]{1,0:T(8,128)(2,1)} %gate_up.1.lhs, bf16[6912,5120]{1,0:T(8,128)(2,1)} %w.3, bf16[128,5120]{1,0:T(8,128)(2,1)} %out_proj.1.x_ref.res_ref), custom_call_target="tpu_custom_call" | custom-call | tf_op jit(solution)/shard_map/down_proj/pallas_call | solution.py:401
  507.0 2.5 copy.74
  (33 shorter events, 5.5 us)
Async XLA Ops:
  102.9 3.4 copy-start
  103.7 19.1 %collective-permute-start.1 = (bf16[512,2,128]{0,2,1:T(8,128)(2,1)}, bf16[512,2,128]{0,2,1:T(8,128)(2,1)}, u32[]{:S(2)}, u32[]{:S(2)}) collective-permute-start(bf16[512,2,128]{0,2,1:T(8,128)(2,1)} %copy.46), channel_id=1, source_target_pairs={{0,1},{1,2},{2,3},{3,0},{4,5},{5,6},{6,7},{7,4},{8,9},{9,10},{10,1... | collective-permute-start | bytes 786440 | tf_op jit(solution)/shard_map/ppermute | solution.py:483
  108.2 14.5 %collective-permute-start = (bf16[512,2,128]{2,0,1:T(8,128)(2,1)}, bf16[512,2,128]{2,0,1:T(8,128)(2,1)}, u32[]{:S(2)}, u32[]{:S(2)}) collective-permute-start(bf16[512,2,128]{2,0,1:T(8,128)(2,1)} %pad_maximum_fusion.1), channel_id=1, source_target_pairs={{0,1},{1,2},{2,3},{3,0},{4,5},{5,6},{6,7},{7,4},{8,9},{9,10},{10,1... | collective-permute-start | bytes 786440 | tf_op jit(solution)/shard_map/ppermute | solution.py:482
  116.1 6.1 %copy-start.2 = (bf16[5120]{0:T(1024)(128)(2,1)S(1)}, bf16[5120]{0:T(1024)(128)(2,1)}, u32[]{:S(2)}) copy-start(bf16[5120]{0:T(1024)(128)(2,1)} %param.15) | copy-start | bytes 30724
  122.8 7.4 %collective-permute-start.3 = (bf16[512,2,128]{0,2,1:T(8,128)(2,1)}, bf16[512,2,128]{0,2,1:T(8,128)(2,1)}, u32[]{:S(2)}, u32[]{:S(2)}) collective-permute-start(bf16[512,2,128]{0,2,1:T(8,128)(2,1)} %collective-permute-done.1), channel_id=1, source_target_pairs={{0,1},{1,2},{2,3},{3,0},{4,5},{5,6},{6,7},{7,4},{8,9},{9,10},{10,1... | collective-permute-start | bytes 786440 | tf_op jit(solution)/shard_map/ppermute | solution.py:483
  122.8 8.6 %collective-permute-start.2 = (bf16[512,2,128]{2,0,1:T(8,128)(2,1)}, bf16[512,2,128]{2,0,1:T(8,128)(2,1)S(1)}, u32[]{:S(2)}, u32[]{:S(2)}) collective-permute-start(bf16[512,2,128]{2,0,1:T(8,128)(2,1)} %collective-permute-done), channel_id=1, source_target_pairs={{0,1},{1,2},{2,3},{3,0},{4,5},{5,6},{6,7},{7,4},{8,9},{9,10},{10,1... | collective-permute-start | bytes 786440 | tf_op jit(solution)/shard_map/ppermute | solution.py:482
  130.1 58.6 %collective-permute-start.5 = (bf16[512,2,128]{0,2,1:T(8,128)(2,1)}, bf16[512,2,128]{0,2,1:T(8,128)(2,1)}, u32[]{:S(2)}, u32[]{:S(2)}) collective-permute-start(bf16[512,2,128]{0,2,1:T(8,128)(2,1)} %collective-permute-done.3), channel_id=1, source_target_pairs={{0,1},{1,2},{2,3},{3,0},{4,5},{5,6},{6,7},{7,4},{8,9},{9,10},{10,1... | collective-permute-start | bytes 786440 | tf_op jit(solution)/shard_map/ppermute | solution.py:483
  131.4 16.3 %collective-permute-start.4 = (bf16[512,2,128]{2,0,1:T(8,128)(2,1)S(1)}, bf16[512,2,128]{2,0,1:T(8,128)(2,1)S(1)}, u32[]{:S(2)}, u32[]{:S(2)}) collective-permute-start(bf16[512,2,128]{2,0,1:T(8,128)(2,1)S(1)} %collective-permute-done.2), channel_id=1, source_target_pairs={{0,1},{1,2},{2,3},{3,0},{4,5},{5,6},{6,7},{7,4},{8,9},{9,10},{10,1... | collective-permute-start | bytes 786440 | tf_op jit(solution)/shard_map/ppermute | solution.py:482
  176.7 8.7 %copy-start.1 = (bf16[512,2,128]{2,1,0:T(2,128)(2,1)S(1)}, bf16[512,2,128]{2,1,0:T(2,128)(2,1)}, u32[]{:S(2)}) copy-start(bf16[512,2,128]{2,1,0:T(2,128)(2,1)} %copy-done) | copy-start | bytes 786436

commit v2 on v1

v2 whole, which is shorter than its diff:
```python
import functools

import jax
import jax.numpy as jnp
from jax import lax
from jax.experimental import pallas as pl
from jax.experimental.pallas import tpu as pltpu
from jax.sharding import PartitionSpec as P

HEAD_DIM = 128
ROPE_BASE = 500000.0
NORM_EPS = 1e-5
NEG_BIG = -1e30
MESH = pl.DeviceIdType.MESH
BF16 = jnp.bfloat16
F32 = jnp.float32
VMEM_LIMIT = 67043328

TP = 4
ROWS = 128
DIM = 5120
KC = 512
NK = DIM // KC
CC = 256
NCC = DIM // CC
PER = KC // CC
HOP = 2
FILL = 2 * HOP + PER
PIECE = ROWS // 2


def tp_signal(z):
    barrier = pltpu.get_barrier_semaphore()
    for peer in range(TP):
        @pl.when(z != peer)
        def _():
            pl.semaphore_signal(barrier, inc=1, device_id={"tp": peer}, device_id_type=MESH)


def tp_wait():
    pl.semaphore_wait(pltpu.get_barrier_semaphore(), TP - 1)


def gather_tools(z, hop, bg, r_right, r_left, s_right, s_left):
    def blk(origin, chunk):
        lane = pl.multiple_of((chunk % PER) * CC, CC)
        return bg.at[chunk // PER, pl.ds(pl.multiple_of(origin * ROWS, ROWS), ROWS), pl.ds(lane, CC)]

    def right(dist, chunk):
        ref = blk(z - dist, chunk)
        return pltpu.make_async_remote_copy(ref, ref, s_right.at[dist, chunk], r_right.at[dist, chunk],
                                            device_id={"tp": jnp.minimum(z + 1, TP - 1)}, device_id_type=MESH)

    def left(dist, chunk):
        ref = blk(z + dist, chunk)
        return pltpu.make_async_remote_copy(ref, ref, s_left.at[dist, chunk], r_left.at[dist, chunk],
                                            device_id={"tp": jnp.maximum(z - 1, 0)}, device_id_type=MESH)

    def got_right(dist, chunk):
        ref = blk(z - 1 - dist, chunk)
        return pltpu.make_async_remote_copy(ref, ref, s_right.at[dist, chunk], r_right.at[dist, chunk],
                                            device_id={"tp": jnp.maximum(z - 1, 0)}, device_id_type=MESH)

    def got_left(dist, chunk):
        ref = blk(z + 1 + dist, chunk)
        return pltpu.make_async_remote_copy(ref, ref, s_left.at[dist, chunk], r_left.at[dist, chunk],
                                            device_id={"tp": jnp.minimum(z + 1, TP - 1)}, device_id_type=MESH)

    def tick(t):
        own = (t >= 0) & (t < NCC)

        @pl.when(own & (z < TP - 1))
        def _():
            right(0, t).start()

        @pl.when(own & (z > 0))
        def _():
            left(0, t).start()

        for d in (1, 2):
            c = t - d * hop
            ok = (c >= 0) & (c < NCC)

            @pl.when(ok & (z < TP - 1) & (z >= d))
            def _():
                got_right(d - 1, c).wait_recv()
                right(d, c).start()

            @pl.when(ok & (z > 0) & (z + d <= TP - 1))
            def _():
                got_left(d - 1, c).wait_recv()
                left(d, c).start()

    def arrived(g):
        @pl.when(z == TP - 1)
        def _():
            for d in range(TP - 1):
                for k in range(PER):
                    got_right(d, g * PER + k).wait_recv()

        @pl.when(z == 0)
        def _():
            for d in range(TP - 1):
                for k in range(PER):
                    got_left(d, g * PER + k).wait_recv()

    def drain():
        def body(c, _):
            for d in range(TP - 1):
                @pl.when((z < TP - 1) & (z >= d))
                def _():
                    right(d, c).wait_send()

                @pl.when((z > 0) & (z + d <= TP - 1))
                def _():
                    left(d, c).wait_send()
            return 0
        lax.fori_loop(0, NCC, body, 0)

    return tick, arrived, drain


def norm_into(z, x_ref, gain_ref, bg):
    gain = gain_ref[...].reshape(1, DIM).astype(F32)

    def body(i, _):
        r0 = pl.multiple_of(i * 16, 16)
        wide = x_ref[pl.ds(r0, 16), :].astype(F32)
        inv = lax.rsqrt(jnp.mean(wide * wide, axis=-1, keepdims=True) + NORM_EPS)
        out = (wide * inv * gain).astype(BF16)
        row = pl.multiple_of(z * ROWS + r0, 16)
        for g in range(NK):
            bg[g, pl.ds(row, 16), :] = out[:, g * KC:(g + 1) * KC]
        return 0
    lax.fori_loop(0, ROWS // 16, body, 0)


GATHER_SEMS = [pltpu.SemaphoreType.DMA((TP - 1, NCC))] * 4

QT = 2304
SLOTS = 3
FINAL = 3
MID_HOP = 1
LAG = 8
AG_AT = 0


def mid_kernel(n_tiles, o_ref, x_ref, gain_ref, wo, wg, wu, out, h_ref, bg, part, from_left, from_right, acc, wbuf, wobuf, norm_b, ss, ratio,
               wsem, wosem, osem, r_right, r_left, s_right, s_left, p_right, p_left, p_send):
    z = lax.axis_index("tp")
    total = NK * 2 * n_tiles

    def fetch(i, start):
        q = i % (2 * n_tiles)
        k0 = pl.multiple_of((i // (2 * n_tiles)) * KC, KC)
        n0 = pl.multiple_of((q % n_tiles) * QT, QT)
        slot = i % SLOTS

        @pl.when(q < n_tiles)
        def _():
            c = pltpu.make_async_copy(wg.at[pl.ds(k0, KC), pl.ds(n0, QT)], wbuf.at[slot], wsem.at[slot])
            c.start() if start else c.wait()

        @pl.when(q >= n_tiles)
        def _():
            c = pltpu.make_async_copy(wu.at[pl.ds(k0, KC), pl.ds(n0, QT)], wbuf.at[slot], wsem.at[slot])
            c.start() if start else c.wait()

    def fetch_out(c):
        return pltpu.make_async_copy(wo.at[:, pl.ds(pl.multiple_of(c * CC, CC), CC)], wobuf.at[c % 2], wosem.at[c % 2])

    def send_right(c, dest):
        return pltpu.make_async_remote_copy(part.at[c, dest], from_left.at[c, dest - 1], p_send.at[c, dest], p_right.at[c, dest - 1],
                                            device_id={"tp": jnp.minimum(z + 1, TP - 1)}, device_id_type=MESH)

    def send_left(c, dest):
        return pltpu.make_async_remote_copy(part.at[c, dest], from_right.at[c, dest], p_send.at[c, dest], p_left.at[c, dest],
                                            device_id={"tp": jnp.maximum(z - 1, 0)}, device_id_type=MESH)

    def got_left(c, dest):
        return pltpu.make_async_remote_copy(part.at[c, dest], from_left.at[c, dest - 1], p_send.at[c, dest], p_right.at[c, dest - 1],
                                            device_id={"tp": jnp.maximum(z - 1, 0)}, device_id_type=MESH)

    def got_right(c, dest):
        return pltpu.make_async_remote_copy(part.at[c, dest], from_right.at[c, dest], p_send.at[c, dest], p_left.at[c, dest],
                                            device_id={"tp": jnp.minimum(z + 1, TP - 1)}, device_id_type=MESH)

    tp_signal(z)
    fetch_out(0).start()
    fetch_out(1).start()
    for i in range(SLOTS - 1):
        fetch(i, True)
    tick, arrived, drain_gather = gather_tools(z, MID_HOP, bg, r_right, r_left, s_right, s_left)

    def product(t):
        @pl.when(t < NCC)
        def _():
            fetch_out(t).wait()
            prod = jnp.dot(o_ref[...], wobuf[t % 2], preferred_element_type=F32).astype(BF16)
            for dest in range(TP):
                part[t, dest] = prod[dest * ROWS:(dest + 1) * ROWS]

            @pl.when(t + 2 < NCC)
            def _():
                fetch_out(t + 2).start()

    def scatter(t):
        cr = t - z
        ok_r = (cr >= 0) & (cr < NCC)
        cl = t - (TP - 1 - z)
        ok_l = (cl >= 0) & (cl < NCC)
        for k in range(TP - 1):
            dest = TP - 1 - k

            @pl.when(ok_r & (dest > z))
            def _():
                @pl.when(z > 0)
                def _():
                    got_left(cr, dest).wait_recv()
                    part[cr, dest] = (part[cr, dest].astype(F32) + from_left[cr, dest - 1].astype(F32)).astype(BF16)
                send_right(cr, dest).start()

            dst = k

            @pl.when(ok_l & (dst < z))
            def _():
                @pl.when(z < TP - 1)
                def _():
                    got_right(cl, dst).wait_recv()
                    part[cl, dst] = (part[cl, dst].astype(F32) + from_right[cl, dst].astype(F32)).astype(BF16)
                send_left(cl, dst).start()

        cf = t - FINAL

        @pl.when((cf >= 0) & (cf < NCC))
        def _():
            cols = pl.ds(pl.multiple_of(jnp.maximum(cf, 0) * CC, CC), CC)

            @pl.when(z > 0)
            def _():
                got_left(cf, z).wait_recv()
                part[cf, z] = (part[cf, z].astype(F32) + from_left[cf, z - 1].astype(F32)).astype(BF16)

            @pl.when(z < TP - 1)
            def _():
                got_right(cf, z).wait_recv()
                part[cf, z] = (part[cf, z].astype(F32) + from_right[cf, z].astype(F32)).astype(BF16)
            h = (x_ref[:, cols].astype(F32) + part[cf, z].astype(F32)).astype(BF16)
            h_ref[:, cols] = h
            lane = pl.multiple_of((cf % PER) * CC, CC)
            bg[cf // PER, pl.ds(pl.multiple_of(z * ROWS, ROWS), ROWS), pl.ds(lane, CC)] = h

    def normalize(g):
        gain = gain_ref[pl.ds(pl.multiple_of(g * KC, KC), KC)].reshape(1, KC).astype(F32)

        def body(i, _):
            rows = pl.ds(pl.multiple_of(i * ROWS, ROWS), ROWS)
            wide = bg[g, rows, :].astype(F32)
            old = ss[rows, :]
            new = old + jnp.sum(wide * wide, axis=-1, keepdims=True)
            r_old = lax.rsqrt(old / DIM + NORM_EPS)
            r_new = lax.rsqrt(new / DIM + NORM_EPS)
            ss[rows, :] = new
            ratio[rows, :] = jnp.where(r_old > 0.0, r_new / r_old, 0.0)
            norm_b[rows, :] = (wide * r_new[:, :1] * gain).astype(BF16)
            return 0
        lax.fori_loop(0, TP, body, 0)

    ss[...] = jnp.zeros(ss.shape, F32)
    product(0)
    tp_wait()

    def fill(t, _):
        @pl.when(t > 0)
        def _():
            product(t)
        scatter(t)
        tick(t - FINAL)

        @pl.when(t < 2 * n_tiles)
        def _():
            def zero(i, _):
                acc[t, pl.ds(pl.multiple_of(i * 32, 32), 32), :] = jnp.zeros((32, QT), F32)
                return 0
            lax.fori_loop(0, TP * ROWS // 32, zero, 0)
        return 0
    lax.fori_loop(0, LAG, fill, 0)

    def step(u, _):
        t = u + LAG
        g = u // 2
        product(t)
        scatter(t)

        @pl.when(u % 2 == 0)
        def _():
            arrived(g)
            normalize(g)

        def tile(j, _):
            i = u * n_tiles + j
            fetch(i, False)

            @pl.when(i + SLOTS - 1 < total)
            def _():
                fetch(i + SLOTS - 1, True)
            q = i % (2 * n_tiles)
            scale = jnp.concatenate([ratio[...]] * (QT // 128), axis=1)
            acc[q] = acc[q] * scale + jnp.dot(norm_b[...], wbuf[i % SLOTS], preferred_element_type=F32)

            @pl.when(j == AG_AT)
            def _():
                tick(t - FINAL)
            return 0
        lax.fori_loop(0, n_tiles, tile, 0)
        return 0
    lax.fori_loop(0, 2 * NK, step, 0)

    def put(j):
        return pltpu.make_async_copy(wbuf.at[j], out.at[:, pl.ds(j * QT, QT)], osem.at[j])

    for j in range(n_tiles):
        def finish(i, _):
            rows = pl.ds(pl.multiple_of(i * 64, 64), 64)
            wbuf[j, rows, :] = (jax.nn.silu(acc[j, rows, :]) * acc[n_tiles + j, rows, :]).astype(BF16)
            return 0
        lax.fori_loop(0, TP * ROWS // 64, finish, 0)
        put(j).start()
    drain_gather()

    def drain(c, _):
        for dest in range(TP):
            @pl.when(dest > z)
            def _():
                send_right(c, max(dest, 1)).wait_send()

            @pl.when(dest < z)
            def _():
                send_left(c, min(dest, TP - 2)).wait_send()
        return 0
    lax.fori_loop(0, NCC, drain, 0)
    for j in range(n_tiles):
        put(j).wait()


def mid(o, x, gain, wo, wg, wu):
    ffn = wg.shape[1]
    n_tiles = ffn // QT
    vm = pl.BlockSpec(memory_space=pltpu.VMEM)
    hbm = pl.BlockSpec(memory_space=pl.ANY)
    dma = pltpu.SemaphoreType.DMA
    return pl.pallas_call(
        functools.partial(mid_kernel, n_tiles),
        out_shape=(jax.ShapeDtypeStruct((TP * ROWS, ffn), BF16), jax.ShapeDtypeStruct((ROWS, DIM), BF16)),
        in_specs=[vm, vm, vm, hbm, hbm, hbm],
        out_specs=(hbm, vm),
        scratch_shapes=[
            pltpu.VMEM((NK, TP * ROWS, KC), BF16),
            pltpu.VMEM((NCC, TP, ROWS, CC), BF16),
            pltpu.VMEM((NCC, TP - 1, ROWS, CC), BF16),
            pltpu.VMEM((NCC, TP - 1, ROWS, CC), BF16),
            pltpu.VMEM((2 * n_tiles, TP * ROWS, QT), F32),
            pltpu.VMEM((SLOTS, KC, QT), BF16),
            pltpu.VMEM((2, wo.shape[0], CC), BF16),
            pltpu.VMEM((TP * ROWS, KC), BF16),
            pltpu.VMEM((TP * ROWS, 128), F32),
            pltpu.VMEM((TP * ROWS, 128), F32),
            dma((SLOTS,)), dma((2,)), dma((n_tiles,)),
        ] + GATHER_SEMS + [dma((NCC, TP - 1)), dma((NCC, TP - 1)), dma((NCC, TP))],
        compiler_params=pltpu.CompilerParams(collective_id=2, has_side_effects=True, vmem_limit_bytes=VMEM_LIMIT),
        name="out_gate_up",
    )(o, x, gain, wo, wg, wu)


def qkv_kernel(x_ref, gain_ref, pos_ref, freq_ref, wq, wk, wv, q_out, kv_out, pos_out,
               bg, acc, wbuf, pos_all, cos_t, sin_t, wsem, psend, precv, r_right, r_left, s_right, s_left):
    z = lax.axis_index("tp")
    nq, nkv = wq.shape[1], wk.shape[1]

    def fetch(g, start):
        k0 = pl.multiple_of(g * KC, KC)
        slot = g % 2
        for idx, (w, off, width) in enumerate(((wq, 0, nq), (wk, nq, nkv), (wv, nq + nkv, nkv))):
            c = pltpu.make_async_copy(w.at[pl.ds(k0, KC), :], wbuf.at[slot, :, pl.ds(off, width)], wsem.at[slot, idx])
            c.start() if start else c.wait()

    tp_signal(z)
    fetch(0, True)
    fetch(1, True)
    pos_all[z] = jnp.broadcast_to(pos_ref[...].reshape(1, ROWS), (8, ROWS))
    norm_into(z, x_ref, gain_ref, bg)
    tp_wait()
    tick, arrived, drain = gather_tools(z, HOP, bg, r_right, r_left, s_right, s_left)

    def pos_copy(peer, origin):
        return pltpu.make_async_remote_copy(pos_all.at[z], pos_all.at[origin], psend.at[peer], precv.at[origin],
                                            device_id={"tp": peer}, device_id_type=MESH)
    tick(0)
    for peer in range(TP):
        @pl.when(z != peer)
        def _():
            pos_copy(peer, z).start()
    acc[...] = jnp.zeros(acc.shape, F32)
    for t in range(1, FILL):
        tick(t)
    for peer in range(TP):
        @pl.when(z != peer)
        def _():
            pos_copy(peer, z).wait_send()
            pos_copy(peer, peer).wait_recv()
    lane = lax.broadcasted_iota(jnp.int32, (ROWS, HEAD_DIM), 1)
    for t in range(TP):
        wide = jnp.broadcast_to(pos_all[t, 0:1, :].astype(F32), (ROWS, ROWS)).T
        ang = wide * freq_ref[...]
        sin = jnp.sin(ang)
        cos_t[t * ROWS:(t + 1) * ROWS, :] = jnp.cos(ang)
        sin_t[t * ROWS:(t + 1) * ROWS, :] = jnp.where(lane < HEAD_DIM // 2, -sin, sin)
        ints = wide.astype(jnp.int32)
        for half in range(2):
            pos_out[half, t * PIECE:(t + 1) * PIECE, :] = ints[half * PIECE:(half + 1) * PIECE, :]

    def step(g, _):
        for h in range(2):
            tick(g * 2 + h + FILL)
        arrived(g)
        fetch(g, False)
        acc[...] += jnp.dot(bg[g], wbuf[g % 2], preferred_element_type=F32)

        @pl.when(g + 2 < NK)
        def _():
            fetch(g + 2, True)
        return 0
    lax.fori_loop(0, NK, step, 0)
    n_rope = (nq + nkv) // HEAD_DIM
    for head in range((nq + 2 * nkv) // HEAD_DIM):
        val = acc[:, head * HEAD_DIM:(head + 1) * HEAD_DIM]
        if head < n_rope:
            val = val * cos_t[...] + pltpu.roll(val, HEAD_DIM // 2, 1) * sin_t[...]
        val = val.astype(BF16)
        dst, idx = (q_out, head) if head < nq // HEAD_DIM else (kv_out, head - nq // HEAD_DIM)
        for t in range(TP):
            for half in range(2):
                r0 = t * ROWS + half * PIECE
                dst[idx, half, t * PIECE:(t + 1) * PIECE, :] = val[r0:r0 + PIECE, :]
    drain()


def qkv_proj(x, gain, pos, wq, wk, wv):
    width = wq.shape[1] + wk.shape[1] + wv.shape[1]
    nq, nkv = wq.shape[1] // HEAD_DIM, 2 * wk.shape[1] // HEAD_DIM
    vm = pl.BlockSpec(memory_space=pltpu.VMEM)
    hbm = pl.BlockSpec(memory_space=pl.ANY)
    half = HEAD_DIM // 2
    inv_freq = ROPE_BASE ** (-jnp.arange(half, dtype=F32) * (2.0 / HEAD_DIM))
    freq = jnp.concatenate([inv_freq, inv_freq]).reshape(1, HEAD_DIM)
    return pl.pallas_call(
        qkv_kernel,
        out_shape=(jax.ShapeDtypeStruct((nq, 2, TP * PIECE, HEAD_DIM), BF16), jax.ShapeDtypeStruct((nkv, 2, TP * PIECE, HEAD_DIM), BF16),
                   jax.ShapeDtypeStruct((2, TP * PIECE, HEAD_DIM), jnp.int32)),
        in_specs=[vm, vm, vm, vm, hbm, hbm, hbm],
        out_specs=(vm, vm, vm),
        scratch_shapes=[
            pltpu.VMEM((NK, TP * ROWS, KC), BF16),
            pltpu.VMEM((TP * ROWS, width), F32),
            pltpu.VMEM((2, KC, width), BF16),
            pltpu.VMEM((TP, 8, ROWS), jnp.int32),
            pltpu.VMEM((TP * ROWS, HEAD_DIM), F32),
            pltpu.VMEM((TP * ROWS, HEAD_DIM), F32),
            pltpu.SemaphoreType.DMA((2, 3)),
            pltpu.SemaphoreType.DMA((TP,)),
            pltpu.SemaphoreType.DMA((TP,)),
        ] + GATHER_SEMS,
        compiler_params=pltpu.CompilerParams(collective_id=1, has_side_effects=True, vmem_limit_bytes=VMEM_LIMIT),
        name="qkv_proj",
    )(x, gain, pos, freq, wq, wk, wv)


CP = 4
BLK = TP * PIECE
PIECES = 2 * CP * TP


def attend_kernel(q_ref, kv_ref, pos_ref, out_ref, kv_all, bias, m_ref, l_ref, acc, ssem, rsem):
    c = lax.axis_index("cp")
    heads = q_ref.shape[0]
    n_kv = kv_ref.shape[0] // 2
    group = heads // n_kv
    mate = c + 1 - 2 * (c % 2)
    across = (c + 2) % CP
    barrier = pltpu.get_barrier_semaphore()
    for peer in (mate, across):
        pl.semaphore_signal(barrier, inc=1, device_id={"cp": peer}, device_id_type=MESH)
    pl.semaphore_wait(barrier, 2)

    def send(src, block, peer, k):
        return pltpu.make_async_remote_copy(src, kv_all.at[block], ssem.at[k], rsem.at[k], device_id={"cp": peer}, device_id_type=MESH)

    to_across = send(kv_ref, c, across, 0)
    to_mate = send(kv_ref, c, mate, 1)
    to_across.start()
    to_mate.start()
    kv_all[c] = kv_ref[...]
    m_ref[...] = jnp.full(m_ref.shape, NEG_BIG, F32)
    l_ref[...] = jnp.zeros(l_ref.shape, F32)
    acc[...] = jnp.zeros(acc.shape, F32)

    def logical(idx, owner, half):
        early = owner * BLK + idx
        late = (PIECES - 1 - TP * owner - idx // PIECE) * PIECE + idx % PIECE
        return jnp.where(half == 0, early, late)

    def stage(i, _):
        src = jnp.where(i == 0, c, jnp.where(i == 1, mate, jnp.where(i == 2, across, CP - 1 - c)))

        @pl.when(i == 1)
        def _():
            send(kv_ref, mate, mate, 1).wait_recv()

        @pl.when(i == 2)
        def _():
            send(kv_ref, across, across, 0).wait_recv()
            send(kv_all.at[across], across, mate, 2).start()

        @pl.when(i == 3)
        def _():
            send(kv_all.at[across], CP - 1 - c, mate, 2).wait_recv()

        def job(j, _):
            qh = jnp.minimum(j, 1)
            kh = j // 2
            need = (j == 1) | ((j == 0) & (src <= c)) | ((j == 2) & (src >= c))

            @pl.when(need)
            def _():
                row = logical(lax.broadcasted_iota(jnp.int32, (BLK, BLK), 0), c, qh)
                col = logical(lax.broadcasted_iota(jnp.int32, (BLK, BLK), 1), src, kh)
                pos = pos_ref[qh]
                first = row - jnp.concatenate([pos, pos], axis=1)
                bias[...] = jnp.where((col <= row) & (col >= first), 0.0, NEG_BIG)

                def one(h, _):
                    g = h // group
                    s = lax.dot_general(q_ref[h, qh], kv_all[src, g, kh], (((1,), (1,)), ((), ())), preferred_element_type=F32)
                    s = s * (HEAD_DIM ** -0.5) + bias[...]
                    m_old = m_ref[qh, h]
                    m_new = jnp.maximum(m_old, jnp.max(s, axis=1, keepdims=True))
                    e = jnp.exp(s - jnp.concatenate([m_new, m_new], axis=1))
                    fac = jnp.exp(m_old - m_new)
                    m_ref[qh, h] = m_new
                    l_ref[qh, h] = l_ref[qh, h] * fac + jnp.sum(e, axis=1, keepdims=True)
                    acc[qh, h] = acc[qh, h] * fac + jnp.dot(e.astype(BF16), kv_all[src, n_kv + g, kh], preferred_element_type=F32)
                    return 0
                lax.fori_loop(0, heads, one, 0, unroll=UNROLL)
            return 0
        lax.fori_loop(0, 3, job, 0)
        return 0
    lax.fori_loop(0, CP, stage, 0)
    for h in range(heads):
        for half in range(2):
            o = (acc[half, h] / l_ref[half, h]).astype(BF16)
            for t in range(TP):
                r0 = t * ROWS + half * PIECE
                out_ref[r0:r0 + PIECE, h * HEAD_DIM:(h + 1) * HEAD_DIM] = o[t * PIECE:(t + 1) * PIECE, :]
    to_across.wait_send()
    to_mate.wait_send()
    send(kv_all.at[across], across, mate, 2).wait_send()


UNROLL = 10


def attend(q, kv, pos):
    heads = q.shape[0]
    vm = pl.BlockSpec(memory_space=pltpu.VMEM)
    state = pltpu.VMEM((2, heads, BLK, HEAD_DIM), F32)
    return pl.pallas_call(
        attend_kernel,
        out_shape=jax.ShapeDtypeStruct((TP * ROWS, heads * HEAD_DIM), BF16),
        in_specs=[vm, vm, vm],
        out_specs=vm,
        scratch_shapes=[pltpu.VMEM((CP,) + kv.shape, BF16), pltpu.VMEM((BLK, BLK), F32), state, state, state,
                        pltpu.SemaphoreType.DMA((3,)), pltpu.SemaphoreType.DMA((3,))],
        compiler_params=pltpu.CompilerParams(collective_id=5, has_side_effects=True, vmem_limit_bytes=VMEM_LIMIT),
        name="attend",
    )(q, kv, pos)


NC = 256
NN = DIM // NC
DOWN_FINAL = 5


def scatter_kernel(lhs, w, res_ref, out_ref, part, from_left, from_right, wbuf, wsem, r_right, r_left, ssem):
    z = lax.axis_index("tp")

    def fetch(c):
        return pltpu.make_async_copy(w.at[:, pl.ds(pl.multiple_of(c * NC, NC), NC)], wbuf.at[c % 2], wsem.at[c % 2])

    tp_signal(z)
    fetch(0).start()
    fetch(1).start()

    def send_right(c, dest):
        return pltpu.make_async_remote_copy(part.at[c, dest], from_left.at[c, dest - 1], ssem.at[c, dest], r_right.at[c, dest - 1],
                                            device_id={"tp": jnp.minimum(z + 1, TP - 1)}, device_id_type=MESH)

    def send_left(c, dest):
        return pltpu.make_async_remote_copy(part.at[c, dest], from_right.at[c, dest], ssem.at[c, dest], r_left.at[c, dest],
                                            device_id={"tp": jnp.maximum(z - 1, 0)}, device_id_type=MESH)

    def got_left(c, dest):
        return pltpu.make_async_remote_copy(part.at[c, dest], from_left.at[c, dest - 1], ssem.at[c, dest], r_right.at[c, dest - 1],
                                            device_id={"tp": jnp.maximum(z - 1, 0)}, device_id_type=MESH)

    def got_right(c, dest):
        return pltpu.make_async_remote_copy(part.at[c, dest], from_right.at[c, dest], ssem.at[c, dest], r_left.at[c, dest],
                                            device_id={"tp": jnp.minimum(z + 1, TP - 1)}, device_id_type=MESH)

    def product(t):
        @pl.when(t < NN)
        def _():
            fetch(t).wait()
            prod = jnp.dot(lhs[...], wbuf[t % 2], preferred_element_type=F32).astype(BF16)
            for dest in range(TP):
                part[t, dest] = prod[dest * ROWS:(dest + 1) * ROWS]

            @pl.when(t + 2 < NN)
            def _():
                fetch(t + 2).start()

    product(0)
    tp_wait()

    def step(t, _):
        @pl.when(t > 0)
        def _():
            product(t)

        cr = t - z
        ok_r = (cr >= 0) & (cr < NN)
        cl = t - (TP - 1 - z)
        ok_l = (cl >= 0) & (cl < NN)
        for k in range(TP - 1):
            dest = TP - 1 - k

            @pl.when(ok_r & (dest > z))
            def _():
                @pl.when(z > 0)
                def _():
                    got_left(cr, dest).wait_recv()
                    part[cr, dest] = (part[cr, dest].astype(F32) + from_left[cr, dest - 1].astype(F32)).astype(BF16)
                send_right(cr, dest).start()

            dst = k

            @pl.when(ok_l & (dst < z))
            def _():
                @pl.when(z < TP - 1)
                def _():
                    got_right(cl, dst).wait_recv()
                    part[cl, dst] = (part[cl, dst].astype(F32) + from_right[cl, dst].astype(F32)).astype(BF16)
                send_left(cl, dst).start()

        cf = t - DOWN_FINAL

        @pl.when(cf >= 0)
        def _():
            cols = pl.ds(pl.multiple_of(jnp.maximum(cf, 0) * NC, NC), NC)

            @pl.when(z > 0)
            def _():
                got_left(cf, z).wait_recv()
                part[cf, z] = (part[cf, z].astype(F32) + from_left[cf, z - 1].astype(F32)).astype(BF16)

            @pl.when(z < TP - 1)
            def _():
                got_right(cf, z).wait_recv()
                part[cf, z] = (part[cf, z].astype(F32) + from_right[cf, z].astype(F32)).astype(BF16)
            out_ref[:, cols] = (res_ref[:, cols].astype(F32) + part[cf, z].astype(F32)).astype(BF16)
        return 0
    lax.fori_loop(0, NN + DOWN_FINAL, step, 0)

    def drain(c, _):
        for dest in range(TP):
            @pl.when(dest > z)
            def _():
                send_right(c, max(dest, 1)).wait_send()

            @pl.when(dest < z)
            def _():
                send_left(c, min(dest, TP - 2)).wait_send()
        return 0
    lax.fori_loop(0, NN, drain, 0)


def scatter_proj(lhs, w, res, cid, name):
    depth = w.shape[0]
    vm = pl.BlockSpec(memory_space=pltpu.VMEM)
    hbm = pl.BlockSpec(memory_space=pl.ANY)
    return pl.pallas_call(
        scatter_kernel,
        out_shape=jax.ShapeDtypeStruct((ROWS, DIM), BF16),
        in_specs=[vm, hbm, vm],
        out_specs=vm,
        scratch_shapes=[
            pltpu.VMEM((NN, TP, ROWS, NC), BF16),
            pltpu.VMEM((NN, TP - 1, ROWS, NC), BF16),
            pltpu.VMEM((NN, TP - 1, ROWS, NC), BF16),
            pltpu.VMEM((2, depth, NC), BF16),
            pltpu.SemaphoreType.DMA((2,)),
            pltpu.SemaphoreType.DMA((NN, TP - 1)),
            pltpu.SemaphoreType.DMA((NN, TP - 1)),
            pltpu.SemaphoreType.DMA((NN, TP)),
        ],
        compiler_params=pltpu.CompilerParams(collective_id=cid, has_side_effects=True, vmem_limit_bytes=VMEM_LIMIT),
        name=name,
    )(lhs, w, res)


def solution(mesh):
    row_mat = P(('dp', 'cp', 'tp'), None)
    row_vec = P(('dp', 'cp', 'tp'))
    col_split = P(None, 'tp')
    row_split = P('tp', None)

    def local_layer(hidden, positions, doc_ids, attn_gain, mlp_gain, w_query, w_key, w_value, w_out, w_gate, w_up, w_down):
        q, kv, pos = qkv_proj(hidden, attn_gain, positions, w_query, w_key, w_value)
        attn_mix = attend(q, kv, pos)
        gated, residual = mid(attn_mix, hidden, mlp_gain, w_out, w_gate, w_up)
        return scatter_proj(gated, w_down, residual, 4, "down_proj")

    in_specs = (row_mat, row_vec, row_vec, P(None), P(None), col_split, col_split, col_split, row_split, col_split, col_split, row_split)
    return jax.shard_map(local_layer, mesh=mesh, in_specs=in_specs, out_specs=row_mat, check_vma=False)
```

time: 515 us -> 385 us (0.75); the launches traced: 510 us -> 385 us
  matrix products: 43.6 us -> 0 us
  Pallas kernels: 410 us -> 382 us
  other arithmetic: 23.5 us -> 0.6 us
  local copies, waits for them, and re-layouts: 17.5 us -> 2.46 us
  starting transfers between devices: 12.9 us -> 0 us
    pallas_call x2 -> x1, Pallas kernels: 194 us -> 99.6 us  [scatter_proj(): pl.pallas_call(scatter_kernel, out_shape=jax.ShapeDtypeStruct((ROWS, DIM)...]
    pallas_call x2 -> x3, Pallas kernels: 216 us -> 282 us  [the longest x1 161 us: mid(): pl.pallas_call(functools.partial(mid_kernel, n_tiles), out_shape=(jax.Sha...]
    dot_general x8 -> x0, matrix products: 43.6 us -> none  [the longest x4 26.3 us: block_attend(): jnp.einsum('hgqk,khd->hgqd', weights.astype(jnp.bfloat16), val_blk, prefe...]
    reduce_sum x4 -> x0, other arithmetic: 18 us -> none  [block_attend(): row_sum = row_sum * factor + jnp.sum(weights, axis=-1)]
    ppermute x6 -> x0, starting transfers between devices: 12.9 us -> none  [the longest x3 12.9 us: local_layer(): key_blk = lax.ppermute(key_blk, 'cp', ring_perm)]
    slice x6 -> x0, local copies, waits for them, and re-layouts: 7.5 us -> none  [the longest x2 4.03 us: local_layer(): qkv[:, :nq].reshape(row_count, q_local, HEAD_DIM)]
  transfers between devices with their start and end apart: 6 -> 0, of which waited for: 1 -> 0; matrix products, arithmetic and copies ran while one was open for 14% -> 0% of each run, Pallas kernels for 0% -> 0%
where the time goes in v2:
time: 385 us
  Pallas kernels  382 us (99%)
    pallas_call x1, Pallas kernels, mid(): pl.pallas_call(functools.partial(mid_kernel, n_tiles), out_shape=(jax.Sha...  161 us
    pallas_call x1, Pallas kernels, scatter_proj(): pl.pallas_call(scatter_kernel, out_shape=jax.ShapeDtypeStruct((ROWS, DIM)...  99.6 us
    pallas_call x1, Pallas kernels, qkv_proj(): pl.pallas_call(qkv_kernel, out_shape=(jax.ShapeDtypeStruct((nq, 2, TP * P...  97.9 us
    pallas_call x1, Pallas kernels, attend(): pl.pallas_call(attend_kernel, out_shape=jax.ShapeDtypeStruct((TP * ROWS,...  23.5 us

profile of v2, /device:TPU:0, one launch (start us, length us, event | category | flops | bytes accessed | tf_op | source)
XLA Modules:
  0.0 385.2 jit_solution(168441445152683214)
XLA Ops:
  0.0 0.6 maximum_bitcast_fusion.freq_ref
  0.6 97.9 %qkv_proj.1 = (bf16[10,2,256,128]{3,2,1,0:T(8,128)(2,1)}, bf16[4,2,256,128]{3,2,1,0:T(8,128)(2,1)}, s32[2,256,128]{2,1,0:T(8,128)}) custom-call(bf16[128,5120]{1,0:T(8,128)(2,1)} %x_ref.3, bf16[5120]{0:T(1024)(128)(2,1)} %gain_ref.2, s32[128]{0:T(128)} %pos_ref.1, f32[1,128]{1,0:T(1,128)} %maximum_bitcast_fusion.freq_ref, bf16[5120,1280]{1,0:T(8,128)(2,1)} %wq.1, ...), custom_call_target="tpu_custom_call" | custom-call | tf_op jit(solution)/shard_map/qkv_proj/pallas_call | solution.py:456
  98.5 23.5 %attend.1.o_ref = bf16[512,1280]{1,0:T(8,128)(2,1)} custom-call(bf16[10,2,256,128]{3,2,1,0:T(8,128)(2,1)} %get-tuple-element.10.q_ref, bf16[4,2,256,128]{3,2,1,0:T(8,128)(2,1)} %get-tuple-element.11.kv_ref, s32[2,256,128]{2,1,0:T(8,128)} %get-tuple-element.12.pos_ref), custom_call_target="tpu_custom_call" | custom-call | tf_op jit(solution)/shard_map/attend/pallas_call | solution.py:576
  122.0 161.1 %out_gate_up.1 = (bf16[512,6912]{1,0:T(8,128)(2,1)}, bf16[128,5120]{1,0:T(8,128)(2,1)}) custom-call(bf16[512,1280]{1,0:T(8,128)(2,1)} %attend.1.o_ref, bf16[128,5120]{1,0:T(8,128)(2,1)} %x_ref.3, bf16[5120]{0:T(1024)(128)(2,1)} %gain_ref.3, bf16[1280,5120]{1,0:T(8,128)(2,1)} %wo.1, bf16[5120,6912]{1,0:T(8,128)(2,1)} %wg.1, bf16[5120,6912]{1,0:T(8,128)(2,1)} %wu.1), custom_call_target="tpu_custom_call" | custom-call | tf_op jit(solution)/shard_map/out_gate_up/pallas_call | solution.py:352
  283.1 99.6 %down_proj.1 = bf16[128,5120]{1,0:T(8,128)(2,1)} custom-call(bf16[512,6912]{1,0:T(8,128)(2,1)} %get-tuple-element.13.lhs, bf16[6912,5120]{1,0:T(8,128)(2,1)} %w.1, bf16[128,5120]{1,0:T(8,128)(2,1)} %get-tuple-element.14.res_ref), custom_call_target="tpu_custom_call" | custom-call | tf_op jit(solution)/shard_map/down_proj/pallas_call | solution.py:700
  382.8 2.5 copy.13
  (1 shorter events, 0.0 us)

commit v3 on v2

--- a/solution.py
+++ b/solution.py
@@ -271,10 +271,8 @@
     tp_wait()
 
     def fill(t, _):
-        @pl.when(t > 0)
-        def _():
-            product(t)
         scatter(t)
+        product(t + 1)
         tick(t - FINAL)
 
         @pl.when(t < 2 * n_tiles)
@@ -289,7 +287,6 @@
     def step(u, _):
         t = u + LAG
         g = u // 2
-        product(t)
         scatter(t)
 
         @pl.when(u % 2 == 0)
@@ -311,6 +308,7 @@
             @pl.when(j == AG_AT)
             def _():
                 tick(t - FINAL)
+                product(t + 1)
             return 0
         lax.fori_loop(0, n_tiles, tile, 0)
         return 0
@@ -492,13 +490,19 @@
         pl.semaphore_signal(barrier, inc=1, device_id={"cp": peer}, device_id_type=MESH)
     pl.semaphore_wait(barrier, 2)
 
-    def send(src, block, peer, k):
-        return pltpu.make_async_remote_copy(src, kv_all.at[block], ssem.at[k], rsem.at[k], device_id={"cp": peer}, device_id_type=MESH)
-
-    to_across = send(kv_ref, c, across, 0)
-    to_mate = send(kv_ref, c, mate, 1)
-    to_across.start()
-    to_mate.start()
+    def half_copy(src, block, peer, half, k):
+        return pltpu.make_async_remote_copy(src.at[:, half], kv_all.at[block, :, half], ssem.at[k], rsem.at[k],
+                                            device_id={"cp": peer}, device_id_type=MESH)
+
+    def mate_copy(block, peer):
+        return pltpu.make_async_remote_copy(kv_ref, kv_all.at[block], ssem.at[4], rsem.at[4], device_id={"cp": peer}, device_id_type=MESH)
+
+    def relay(half):
+        return half_copy(kv_all.at[across], across, mate, half, 2 + half)
+
+    for half in range(2):
+        half_copy(kv_ref, c, across, half, half).start()
+    mate_copy(c, mate).start()
     kv_all[c] = kv_ref[...]
     m_ref[...] = jnp.full(m_ref.shape, NEG_BIG, F32)
     l_ref[...] = jnp.zeros(l_ref.shape, F32)
@@ -510,25 +514,28 @@
         return jnp.where(half == 0, early, late)
 
     def stage(i, _):
-        src = jnp.where(i == 0, c, jnp.where(i == 1, mate, jnp.where(i == 2, across, CP - 1 - c)))
+        diag = CP - 1 - c
+        src = jnp.where(i == 0, c, jnp.where(i == 1, mate, jnp.where(i % 2 == 0, across, diag)))
 
         @pl.when(i == 1)
         def _():
-            send(kv_ref, mate, mate, 1).wait_recv()
-
-        @pl.when(i == 2)
-        def _():
-            send(kv_ref, across, across, 0).wait_recv()
-            send(kv_all.at[across], across, mate, 2).start()
-
-        @pl.when(i == 3)
-        def _():
-            send(kv_all.at[across], CP - 1 - c, mate, 2).wait_recv()
+            mate_copy(mate, mate).wait_recv()
+
+        for half in range(2):
+            @pl.when(i == 2 + 2 * half)
+            def _():
+                half_copy(kv_ref, across, across, half, half).wait_recv()
+                relay(half).start()
+
+            @pl.when(i == 3 + 2 * half)
+            def _():
+                half_copy(kv_all.at[across], diag, mate, half, 2 + half).wait_recv()
 
         def job(j, _):
             qh = jnp.minimum(j, 1)
             kh = j // 2
-            need = (j == 1) | ((j == 0) & (src <= c)) | ((j == 2) & (src >= c))
+            early, late = i < CP, (i < 2) | (i >= CP)
+            need = (early & (j == 1)) | (early & (j == 0) & (src <= c)) | (late & (j == 2) & (src >= c))
 
             @pl.when(need)
             def _():
@@ -554,16 +561,17 @@
             return 0
         lax.fori_loop(0, 3, job, 0)
         return 0
-    lax.fori_loop(0, CP, stage, 0)
+    lax.fori_loop(0, CP + 2, stage, 0)
     for h in range(heads):
         for half in range(2):
             o = (acc[half, h] / l_ref[half, h]).astype(BF16)
             for t in range(TP):
                 r0 = t * ROWS + half * PIECE
                 out_ref[r0:r0 + PIECE, h * HEAD_DIM:(h + 1) * HEAD_DIM] = o[t * PIECE:(t + 1) * PIECE, :]
-    to_across.wait_send()
-    to_mate.wait_send()
-    send(kv_all.at[across], across, mate, 2).wait_send()
+    for half in range(2):
+        half_copy(kv_ref, c, across, half, half).wait_send()
+        relay(half).wait_send()
+    mate_copy(c, mate).wait_send()
 
 
 UNROLL = 10
@@ -579,7 +587,7 @@
         in_specs=[vm, vm, vm],
         out_specs=vm,
         scratch_shapes=[pltpu.VMEM((CP,) + kv.shape, BF16), pltpu.VMEM((BLK, BLK), F32), state, state, state,
-                        pltpu.SemaphoreType.DMA((3,)), pltpu.SemaphoreType.DMA((3,))],
+                        pltpu.SemaphoreType.DMA((5,)), pltpu.SemaphoreType.DMA((5,))],
         compiler_params=pltpu.CompilerParams(collective_id=5, has_side_effects=True, vmem_limit_bytes=VMEM_LIMIT),
         name="attend",
     )(q, kv, pos)

time: 385 us -> 382 us (level)
  no operation moved by 1% of the time
where the time goes in v3:
time: 382 us
  Pallas kernels  379 us (99%)
    pallas_call x1, Pallas kernels, mid(): pl.pallas_call(functools.partial(mid_kernel, n_tiles), out_shape=(jax.Sha...  161 us
    pallas_call x1, Pallas kernels, scatter_proj(): pl.pallas_call(scatter_kernel, out_shape=jax.ShapeDtypeStruct((ROWS, DIM)...  100 us
    pallas_call x1, Pallas kernels, qkv_proj(): pl.pallas_call(qkv_kernel, out_shape=(jax.ShapeDtypeStruct((nq, 2, TP * P...  97.9 us
    pallas_call x1, Pallas kernels, attend(): pl.pallas_call(attend_kernel, out_shape=jax.ShapeDtypeStruct((TP * ROWS,...  20.4 us

profile of v3, /device:TPU:0, one launch (start us, length us, event | category | flops | bytes accessed | tf_op | source)
XLA Modules:
  0.0 382.2 jit_solution(10110242446906193220)
XLA Ops:
  0.0 0.6 maximum_bitcast_fusion.freq_ref
  0.6 97.9 %qkv_proj.1 = (bf16[10,2,256,128]{3,2,1,0:T(8,128)(2,1)}, bf16[4,2,256,128]{3,2,1,0:T(8,128)(2,1)}, s32[2,256,128]{2,1,0:T(8,128)}) custom-call(bf16[128,5120]{1,0:T(8,128)(2,1)} %x_ref.3, bf16[5120]{0:T(1024)(128)(2,1)} %gain_ref.2, s32[128]{0:T(128)} %pos_ref.1, f32[1,128]{1,0:T(1,128)} %maximum_bitcast_fusion.freq_ref, bf16[5120,1280]{1,0:T(8,128)(2,1)} %wq.1, ...), custom_call_target="tpu_custom_call" | custom-call | tf_op jit(solution)/shard_map/qkv_proj/pallas_call | solution.py:454
  98.5 20.4 %attend.1.o_ref = bf16[512,1280]{1,0:T(8,128)(2,1)} custom-call(bf16[10,2,256,128]{3,2,1,0:T(8,128)(2,1)} %get-tuple-element.10.q_ref, bf16[4,2,256,128]{3,2,1,0:T(8,128)(2,1)} %get-tuple-element.11.kv_ref, s32[2,256,128]{2,1,0:T(8,128)} %get-tuple-element.12.pos_ref), custom_call_target="tpu_custom_call" | custom-call | tf_op jit(solution)/shard_map/attend/pallas_call | solution.py:584
  118.9 160.6 %out_gate_up.1 = (bf16[512,6912]{1,0:T(8,128)(2,1)}, bf16[128,5120]{1,0:T(8,128)(2,1)}) custom-call(bf16[512,1280]{1,0:T(8,128)(2,1)} %attend.1.o_ref, bf16[128,5120]{1,0:T(8,128)(2,1)} %x_ref.3, bf16[5120]{0:T(1024)(128)(2,1)} %gain_ref.3, bf16[1280,5120]{1,0:T(8,128)(2,1)} %wo.1, bf16[5120,6912]{1,0:T(8,128)(2,1)} %wg.1, bf16[5120,6912]{1,0:T(8,128)(2,1)} %wu.1), custom_call_target="tpu_custom_call" | custom-call | tf_op jit(solution)/shard_map/out_gate_up/pallas_call | solution.py:350
  279.5 100.2 %down_proj.1 = bf16[128,5120]{1,0:T(8,128)(2,1)} custom-call(bf16[512,6912]{1,0:T(8,128)(2,1)} %get-tuple-element.13.lhs, bf16[6912,5120]{1,0:T(8,128)(2,1)} %w.1, bf16[128,5120]{1,0:T(8,128)(2,1)} %get-tuple-element.14.res_ref), custom_call_target="tpu_custom_call" | custom-call | tf_op jit(solution)/shard_map/down_proj/pallas_call | solution.py:708
  379.8 2.5 copy.13
  (1 shorter events, 0.0 us)
